TPU v7x, 32 devices: a whole 2x2x4 slice. The times are simulated.
32 devices in a mesh: tile: 2 (over y), seq: 4 (over z), group: 4 (over x, core).
Axes of the slice: x: 2, y: 2, z: 4, core: 2. Of those that a mesh axis runs over, the one named last changes fastest.
Arguments:
- features: bfloat16 [4, 4, 2, 8, 64, 512], P('seq', 'group', None, 'tile'), may hold values from -6 to 6
- conv_weight: bfloat16 [3, 3, 3, 512, 16], replicated, may hold values from -0.0546875 to 0.0546875
- conv_bias: float32 [16], replicated, may hold values from -3 to 3
- embed_qkv: bfloat16 [64, 4608], replicated, may hold values from -0.75 to 0.75
- query_gain: float32 [128], replicated, may hold values from 0.5 to 2
- key_gain: float32 [128], replicated, may hold values from 0.5 to 2
- bucket: int32 [4, 4], replicated, may hold values from 0 to 3, as said below
- frames: int32 [4, 4], replicated, may hold values from 1 to 2
Outputs:
- attended: bfloat16 [4, 4, 2, 256, 1536], P('seq', 'group', None, 'tile')
Inputs may be any that keep to these rules, and one draw needn't show every extreme that they name: In each row every bucket receives at most 2 clips; exactly 1 buckets receive 2, and as many receive none.
All inputs are finite; a program needn't handle non-finite values.
Results may differ from a plain program's by a relative error of at most 0.0046.
Values may be sent and summed in bfloat16 or wider, within the bound.
No kernel may reach another device: no remote copies, remote signals or barrier semaphores. Data moves between devices by JAX's collectives and lax.ppermute only.
A program may use at most 128 MiB of HBM per device.

v0:
```python
import math

import jax
import jax.numpy as jnp
from jax import lax
from jax.sharding import PartitionSpec as P

HEADS = 12
HEAD = 128
D = 1536
CAP = 2


def with_halo(block, sides, width):
    for axis, dim in sides:
        count = lax.axis_size(axis)
        forward = [(i, i + 1) for i in range(count - 1)]
        backward = [(target, source) for source, target in forward]
        low = lax.ppermute(
            lax.slice_in_dim(block, block.shape[dim] - width, None, axis=dim), axis, forward
        )
        high = lax.ppermute(lax.slice_in_dim(block, 0, width, axis=dim), axis, backward)
        block = jnp.concatenate([low, block, high], axis=dim)
    return block


def tap_products(padded, conv_weight):
    channels = padded.shape[-1]
    flat_weight = jnp.transpose(conv_weight, (3, 0, 1, 2, 4)).reshape(channels, -1)
    products = jnp.dot(
        padded.reshape(-1, channels), flat_weight, preferred_element_type=jnp.float32
    )
    return products.reshape(padded.shape[:-1] + (27, conv_weight.shape[-1]))


def tap_sum(products, frame_count, row_count, col_count):
    running = jnp.zeros((frame_count, row_count, col_count, products.shape[-1]), jnp.float32)
    for depth_tap in range(3):
        for row_tap in range(3):
            for col_tap in range(3):
                tap_index = depth_tap * 9 + row_tap * 3 + col_tap
                running = (
                    running
                    + products[
                        depth_tap : depth_tap + frame_count,
                        row_tap : row_tap + row_count,
                        col_tap : col_tap + col_count,
                        tap_index,
                    ]
                )
    return running


def head_norm(values, gain_vec, head_size):
    shaped = values.reshape(values.shape[:-1] + (-1, head_size))
    scaled = shaped * lax.rsqrt(jnp.mean(shaped * shaped, axis=-1, keepdims=True) + 1e-06)
    return scaled * gain_vec


def attend(queries, key_rows, value_rows, key_valid):
    scores = jnp.einsum("qhe,khe->hqk", queries, key_rows, preferred_element_type=jnp.float32)
    scores = jnp.where(key_valid[None, None, :], scores, -1e30)
    row_max = jnp.max(scores, axis=-1, keepdims=True)
    weights = jnp.exp(scores - row_max)
    totals = jnp.sum(weights, axis=-1)
    mixed_out = jnp.einsum(
        "hqk,khe->qhe", weights.astype(jnp.bfloat16), value_rows, preferred_element_type=jnp.float32
    )
    return mixed_out / jnp.transpose(totals)[:, :, None]


def shards(features, conv_weight, conv_bias, embed_qkv, query_gain, key_gain, bucket, frames):
    local_block = features[0, 0]
    frame_count, row_count, col_count, channels = local_block.shape
    tile_here = lax.axis_index("tile")
    is_first = tile_here == 0
    is_last = tile_here == lax.axis_size("tile") - 1
    extended = with_halo(local_block, (("tile", 1),), 1)
    extended = extended.at[:, 0].set(jnp.where(is_first, local_block[:, 0], extended[:, 0]))
    extended = extended.at[:, row_count + 1].set(
        jnp.where(is_last, local_block[:, row_count - 1], extended[:, row_count + 1])
    )
    padded = jnp.pad(extended, ((2, 0), (0, 0), (1, 1), (0, 0)), mode="edge")
    summed = tap_sum(tap_products(padded, conv_weight), frame_count, row_count, col_count)
    latent = (summed + conv_bias).astype(jnp.bfloat16)
    latent_channels = latent.shape[-1]
    tokens = latent.reshape(frame_count, row_count // 2, 2, col_count // 2, 2, latent_channels)
    tokens = jnp.transpose(tokens, (0, 1, 3, 2, 4, 5)).reshape(-1, 4 * latent_channels)
    groups = lax.axis_size("group")
    group_here = lax.axis_index("group")
    bucket_row = lax.dynamic_index_in_dim(bucket, lax.axis_index("seq"), 0, keepdims=False)
    frame_row = lax.dynamic_index_in_dim(frames, lax.axis_index("seq"), 0, keepdims=False)
    order_ids = jnp.arange(groups, dtype=jnp.int32)
    same_bucket = bucket_row[:, None] == bucket_row[None, :]
    earlier = order_ids[None, :] < order_ids[:, None]
    slot_of = jnp.sum(jnp.where(same_bucket & earlier, 1, 0), axis=1).astype(jnp.int32)
    slot_ids = jnp.arange(CAP, dtype=jnp.int32)
    picked = (bucket_row[None, :] == group_here) & (slot_of[None, :] == slot_ids[:, None])
    selector = picked.astype(jnp.bfloat16)
    filled = jnp.sum(jnp.where(picked, 1, 0), axis=1)
    slot_frames = jnp.sum(jnp.where(picked, frame_row[None, :], 0), axis=1)
    gathered = jnp.einsum(
        "cg,gtf->ctf",
        selector,
        lax.all_gather(tokens[None], "group", axis=0, tiled=True),
        preferred_element_type=jnp.float32,
    )
    slots = gathered.astype(jnp.bfloat16)
    query_weight = embed_qkv[:, :D]
    pair_weight = embed_qkv[:, D:]
    flat_rows = lax.all_gather(slots, "tile", axis=1, tiled=True)
    projected = jnp.einsum(
        "ctf,fe->cte", flat_rows, pair_weight, preferred_element_type=jnp.float32
    )
    normed = (
        head_norm(projected[..., :D], key_gain, HEAD)
        .reshape(projected.shape[:-1] + (D,))
        .astype(jnp.bfloat16)
    )
    key_values = jnp.concatenate([normed, projected[..., D:].astype(jnp.bfloat16)], axis=-1)
    query_full = jnp.einsum("ctf,fe->cte", slots, query_weight, preferred_element_type=jnp.float32)
    queries = (head_norm(query_full, query_gain, HEAD) / math.sqrt(HEAD)).astype(jnp.bfloat16)
    token_count = slots.shape[1]
    per_frame = row_count // 2 * (col_count // 2)
    clip_tokens = key_values.shape[1]
    key_frame = jnp.arange(clip_tokens, dtype=jnp.int32) % token_count // per_frame
    query_frame = jnp.arange(token_count, dtype=jnp.int32) // per_frame
    outputs = []
    for slot_at in range(CAP):
        key_rows = key_values[slot_at, :, :D].reshape(clip_tokens, HEADS, HEAD)
        value_rows = key_values[slot_at, :, D:].reshape(clip_tokens, HEADS, HEAD)
        mixed_out = attend(queries[slot_at], key_rows, value_rows, key_frame < slot_frames[slot_at])
        query_keep = (query_frame < slot_frames[slot_at]) & (filled[slot_at] > 0)
        outputs.append(
            jnp.where(query_keep[:, None], mixed_out.reshape(token_count, D), 0.0).astype(
                jnp.bfloat16
            )
        )
    return jnp.stack(outputs)[None, None]


def solution(mesh):
    in_specs = (P("seq", "group", None, "tile", None, None), P(), P(), P(), P(), P(), P(), P())
    out_specs = P("seq", "group", None, "tile", None)
    return jax.shard_map(shards, mesh=mesh, in_specs=in_specs, out_specs=out_specs, check_vma=False)
```

profile of v0, /device:TPU:0, one launch (start us, length us, event | category | flops | bytes accessed | tf_op | source)
XLA Modules:
  0.0 73.9 jit_solution(16133157785294748377)
XLA Ops:
  0.0 1.1 %fusion.56 = (bf16[2,1,64,512]{3,2,1,0:T(8,128)(2,1)S(1)}, bf16[2,1,64,512]{3,2,1,0:T(8,128)(2,1)S(1)}) fusion(bf16[2,4,64,512]{3,2,1,0:T(8,128)(2,1)} %bitcast.97), kind=kLoop, calls=%fused_computation.113 | loop fusion | bytes 524288 | tf_op jit(solution)/shard_map/slice | solution.py:20
  1.1 1.3 %collective-permute-start.1 = (bf16[2,1,64,512]{3,2,1,0:T(8,128)(2,1)S(1)}, bf16[2,1,64,512]{3,2,1,0:T(8,128)(2,1)S(1)}, u32[]{:S(2)}, u32[]{:S(2)}) collective-permute-start(bf16[2,1,64,512]{3,2,1,0:T(8,128)(2,1)S(1)} %get-tuple-element.46), channel_id=1, source_target_pairs={{16,0},{17,1},{18,2},{19,3},{20,4},{21,5},{22,6},{23,7},{24,8},{25... | collective-permute-start | bytes 393224 | tf_op jit(solution)/shard_map/ppermute | solution.py:22
  2.4 4.9 %collective-permute-start = (bf16[2,1,64,512]{3,2,1,0:T(8,128)(2,1)S(1)}, bf16[2,1,64,512]{3,2,1,0:T(8,128)(2,1)S(1)}, u32[]{:S(2)}, u32[]{:S(2)}) collective-permute-start(bf16[2,1,64,512]{3,2,1,0:T(8,128)(2,1)S(1)} %get-tuple-element.45), channel_id=1, source_target_pairs={{0,16},{1,17},{2,18},{3,19},{4,20},{5,21},{6,22},{7,23},{8,24},{9,... | collective-permute-start | bytes 393224 | tf_op jit(solution)/shard_map/ppermute | solution.py:19
  7.3 0.7 fusion.49
  8.0 0.7 compare_bitcast_fusion
  8.7 0.2 select_reduce_fusion
  8.9 0.7 broadcast_bitcast_fusion
  9.5 0.7 fusion.48
  10.2 0.1 select_reduce_fusion.1
  10.4 0.7 fusion.58
  11.0 0.6 fusion.57
  11.7 1.3 %broadcast_compare_fusion = (pred[256]{0:T(512)(128)(4,1)S(1)}, pred[256]{0:T(512)(128)(4,1)S(1)}) fusion(s32[]{:T(128)} %bitcast.39, s32[]{:T(128)} %bitcast.3), kind=kLoop, calls=%fused_computation.104 | loop fusion | flops 5888 | bytes 520 | tf_op jit(solution)/shard_map/lt | solution.py:132
  14.3 1.3 %compare_and_fusion = (pred[128]{0:T(512)(128)(4,1)S(1)}, pred[128]{0:T(512)(128)(4,1)S(1)}) fusion(pred[]{:T(512)} %bitcast.40, s32[]{:T(128)} %bitcast.39, pred[]{:T(512)} %bitcast.4, s32[]{:T(128)} %bitcast.3), kind=kLoop, calls=%fused_computation.86 | loop fusion | flops 1536 | bytes 266 | tf_op jit(solution)/shard_map/and | solution.py:133
  15.7 1.1 %pad_maximum_fusion = bf16[2,6,64,512]{3,2,1,0:T(8,128)(2,1)S(1)} fusion(bf16[2,1,64,512]{3,2,1,0:T(8,128)(2,1)S(1)} %collective-permute-done.1, bf16[2,4,64,512]{3,2,1,0:T(8,128)(2,1)} %bitcast.98, bf16[2,1,64,512]{3,2,1,0:T(8,128)(2,1)S(1)} %collective-permute-done), kind=kLoop, calls=%fused_computation.39 | loop fusion | flops 786432 | bytes 1572864 | tf_op jit(solution)/shard_map/concatenate | solution.py:23
  17.0 1.9 %fusion.8 = f32[4,6,66,27,16]{2,3,4,1,0:T(8,128)S(1)} fusion(bf16[2,6,64,512]{3,2,1,0:T(8,128)(2,1)S(1)} %fusion.41, bf16[2,6,64,512]{3,2,1,0:T(8,128)(2,1)S(1)} %reshape.268, bf16[27,16,512,1,1]{2,1,0,4,3:T(8,128)(2,1)S(1)} %bitcast.90), kind=kOutput, calls=%fused_computation.12 | convolution fusion | flops 715309056 | bytes 4752384 | tf_op jit(solution)/shard_map/dot_general | solution.py:30
  18.9 1.1 %fusion.53 = (f32[2,4,64,1,16]{2,3,4,1,0:T(1,128)S(1)}, f32[2,4,64,1,16]{2,3,4,1,0:T(1,128)S(1)}, f32[2,4,64,1,16]{2,3,4,1,0:T(1,128)S(1)}, f32[2,4,64,1,16]{2,3...) fusion(f32[4,6,66,27,16]{2,3,4,1,0:T(8,128)S(1)} %fusion.8), kind=kLoop, calls=%fused_computation.110 | loop fusion | bytes 655360 | tf_op jit(solution)/shard_map/slice | solution.py:44
  20.0 1.5 %slice_add_fusion = f32[2,4,64,1,16]{2,3,4,1,0:T(1,128)S(1)} fusion(f32[4,6,66,27,16]{2,3,4,1,0:T(8,128)S(1)} %fusion.8), kind=kLoop, calls=%fused_computation.60 | loop fusion | flops 131072 | bytes 589824 | tf_op jit(solution)/shard_map/add | solution.py:43
  21.6 0.1 copy.86
  21.7 0.1 copy.85
  21.9 0.1 copy.84
  22.0 0.1 copy.83
  22.1 0.1 copy.82
  22.3 0.1 copy.81
  22.4 0.1 copy.80
  22.5 0.1 copy.79
  22.7 0.1 copy.78
  22.8 0.1 copy.76
  22.9 0.1 copy.77
  23.1 0.8 %fusion.42 = bf16[2,2,32,2,2,16]{5,4,2,3,1,0:T(2,128)(2,1)S(1)} fusion(f32[16]{0:T(128)S(1)} %copy-done.9, f32[2,2,2,32,2,16]{5,4,3,2,1,0:T(2,128)S(1)} %bitcast.101, f32[2,2,2,32,2,16]{5,4,3,2,1,0:T(2,128)S(1)} %bitcast.102, f32[2,2,2,32,2,16]{5,4,3,2,1,0:T(2,128)S(1)} %bitcast.103, f32[2,2,2,32,2,16]{5,4,3,2,1,0:T(2,128)S(1)} %bitcast.104, ...), kind=kLoop, calls=%fused_computation.59 | loop fusion | flops 98304 | bytes 376896 | tf_op jit(solution)/shard_map/transpose | solution.py:88
  23.9 0.1 copy.87
  24.2 5.8 %all_gather.6 = bf16[4,128,64]{1,2,0:T(8,128)(2,1)S(1)} all-gather(bf16[1,128,64]{1,2,0:T(8,128)(2,1)S(1)} %broadcast_in_dim_reshape.3), channel_id=1, replica_groups=mesh['tile'=2,'seq'=4,'group'=4] {'group'}, dimensions={0}, use_global_device_ids=true | all-gather | bytes 81920 | tf_op jit(solution)/shard_map/all_gather | solution.py:105
  30.0 0.2 convolution_convert_fusion
  30.2 4.8 %all_gather.7 = bf16[2,256,64]{1,0,2:T(2,128)(2,1)S(1)} all-gather(bf16[2,128,64]{1,0,2:T(2,128)(2,1)S(1)} %convolution_convert_fusion), channel_id=1, replica_groups=mesh['tile'=2,'seq'=4,'group'=4] {'tile'}, dimensions={1}, use_global_device_ids=true | all-gather | bytes 98304 | tf_op jit(solution)/shard_map/all_gather | solution.py:111
  34.9 1.3 %fusion.38 = f32[2,128,1536]{1,2,0:T(8,128)S(1)} fusion(bf16[64,4608]{1,0:T(8,128)(2,1)} %param.15, bf16[2,128,64]{1,0,2:T(2,128)(2,1)S(1)} %convolution_convert_fusion), kind=kOutput, calls=%fused_computation.53 | convolution fusion | flops 50331648 | bytes 1802240 | tf_op jit(solution)/shard_map/ctf,fe->cte/dot_general | solution.py:121
  36.3 1.7 %copy.93 = f32[2,128,12,128]{3,1,2,0:T(8,128)} copy(f32[2,128,12,128]{1,3,2,0:T(8,128)S(1)} %bitcast.91) | data formatting | bytes 3145728 | tf_op jit(solution)/shard_map/reshape | solution.py:55
  38.0 0.1 multiply_reduce_fusion
  38.1 3.7 %fusion.59 = (bf16[2,256,3072]{2,1,0:T(8,128)(2,1)S(1)}, f32[2,256,3072]{2,1,0:T(8,128)}) fusion(bf16[64,4608]{1,0:T(8,128)(2,1)S(1)} %copy-done.8, bf16[2,256,64]{1,0,2:T(2,128)(2,1)S(1)} %all_gather.7), kind=kOutput, calls=%fused_computation.116 | convolution fusion | flops 202899456 | bytes 9895936 | tf_op jit(solution)/shard_map/ctf,fe->cte/dot_general | solution.py:112
  41.8 1.0 %fusion.54 = (bf16[1,256,1536]{2,1,0:T(8,128)(2,1)}, bf16[1,256,1536]{2,1,0:T(8,128)(2,1)S(1)}) fusion(bf16[2,256,3072]{2,1,0:T(8,128)(2,1)S(1)} %get-tuple-element.51), kind=kLoop, calls=%fused_computation.111 | loop fusion | bytes 3145728 | tf_op jit(solution)/shard_map/slice | solution.py:131
  42.7 1.1 %copy.99 = bf16[1,256,1536]{1,2,0:T(8,128)(2,1)} copy(bf16[1,256,1536]{2,1,0:T(8,128)(2,1)S(1)} %get-tuple-element.42) | data formatting | bytes 1572864 | tf_op jit(solution)/shard_map/slice | solution.py:131
  43.9 3.8 %slice_multiply_fusion = f32[2,256,1536]{2,1,0:T(8,128)} fusion(f32[2,256,3072]{2,1,0:T(8,128)} %get-tuple-element.52), kind=kLoop, calls=%fused_computation.7 | loop fusion | flops 786432 | bytes 6291456 | tf_op jit(solution)/shard_map/mul | solution.py:56
  47.7 3.5 %copy.94 = f32[2,256,1536]{1,2,0:T(8,128)} copy(f32[2,256,1536]{2,1,0:T(8,128)} %slice_multiply_fusion) | data formatting | bytes 6291456 | tf_op jit(solution)/shard_map/mul | solution.py:56
  51.2 2.1 %reduce_sum.67 = f32[2,256,12]{1,2,0:T(8,128)S(1)} reduce(f32[2,256,12,128]{1,3,2,0:T(8,128)} %bitcast.93, f32[]{:T(128)} %constant.134.clone.1), dimensions={3}, to_apply=%region_4.5 | reduce | flops 780288 | bytes 3170308 | tf_op jit(solution)/shard_map/reduce_sum | solution.py:56
  53.4 1.9 %mul.56 = f32[2,256,12,128]{1,3,2,0:T(8,128)} broadcast(f32[2,256,12]{1,2,0:T(8,128)S(1)} %add_rsqrt_fusion), dimensions={0,1,2} | broadcast | bytes 3170304 | tf_op jit(solution)/shard_map/mul | solution.py:56
  55.3 3.6 %copy.95 = f32[2,256,1536]{2,1,0:T(8,128)} copy(f32[2,256,1536]{1,2,0:T(8,128)} %bitcast.94) | data formatting | bytes 6291456 | tf_op jit(solution)/shard_map/mul | solution.py:56
  58.8 3.6 %multiply_convert_fusion = bf16[2,256,1536]{2,1,0:T(8,128)(2,1)S(1)} fusion(f32[2,256,1536]{2,1,0:T(8,128)} %copy.95, f32[2,256,3072]{2,1,0:T(8,128)} %get-tuple-element.52, f32[1536]{0:T(1024)S(1)} %broadcast_bitcast_fusion), kind=kLoop, calls=%fused_computation.6 | loop fusion | flops 2359296 | bytes 7870464 | tf_op jit(solution)/shard_map/convert_element_type | solution.py:118
  62.5 1.0 %fusion.55 = (bf16[1,256,1536]{2,1,0:T(8,128)(2,1)}, bf16[1,256,1536]{2,1,0:T(8,128)(2,1)S(1)}) fusion(bf16[2,256,1536]{2,1,0:T(8,128)(2,1)S(1)} %multiply_convert_fusion), kind=kLoop, calls=%fused_computation.112 | loop fusion | bytes 3145728 | tf_op jit(solution)/shard_map/slice | solution.py:130
  63.4 1.2 %copy.100 = bf16[1,256,1536]{1,2,0:T(8,128)(2,1)} copy(bf16[1,256,1536]{2,1,0:T(8,128)(2,1)S(1)} %get-tuple-element.44) | data formatting | bytes 1572864 | tf_op jit(solution)/shard_map/slice | solution.py:130
  64.6 0.5 multiply_convert_fusion.1
  65.1 0.6 copy-done.4
  65.7 0.4 fusion.60
  66.2 0.5 fusion.25
  66.7 0.2 copy-done.6
  66.9 1.2 %fusion.28 = bf16[128,12,128]{0,2,1:T(8,128)(2,1)} fusion(bf16[256,12,128]{0,2,1:T(8,128)(2,1)S(1)} %bitcast.112, f32[12,128,256]{2,1,0:T(8,128)S(1)} %get-tuple-element.54, f32[12,128]{1,0:T(8,128)S(1)} %get-tuple-element.53, f32[128,12]{0,1:T(8,128)S(1)} %bitcast.116), kind=kOutput, calls=%fused_computation.36 | convolution fusion | flops 101842944 | bytes 2764800 | tf_op jit(solution)/shard_map/hqk,khe->qhe/dot_general | solution.py:66
  68.1 1.2 %copy.102 = bf16[1,128,1536]{2,1,0:T(8,128)(2,1)S(1)} copy(bf16[1,128,1536]{1,2,0:T(8,128)(2,1)} %bitcast.114) | data formatting | bytes 786432 | tf_op jit(solution)/shard_map/reshape | solution.py:135
  69.4 1.2 %copy.90 = bf16[1,256,1536]{1,2,0:T(8,128)(2,1)} copy(bf16[1,256,1536]{2,1,0:T(8,128)(2,1)S(1)} %copy-done.2) | data formatting | bytes 1572864 | tf_op jit(solution)/shard_map/slice | solution.py:131
  70.5 0.3 copy.96
  70.8 0.4 fusion.61
  71.3 0.5 fusion.23
  71.8 0.2 copy-done.7
  72.0 0.5 fusion.27
  72.5 0.2 copy.98
  72.6 0.1 select_convert_fusion
  72.8 0.1 select_convert_fusion.1
  72.9 0.9 %maximum_bitcast_fusion = bf16[1,1,2,128,1536]{4,3,2,1,0:T(8,128)(2,1)} fusion(bf16[1,128,1536]{2,1,0:T(8,128)(2,1)S(1)} %select_convert_fusion, bf16[1,128,1536]{2,1,0:T(8,128)(2,1)S(1)} %select_convert_fusion.1), kind=kLoop, calls=%fused_computation.40 | loop fusion | flops 393216 | bytes 1572864 | tf_op jit(solution)/shard_map/broadcast_in_dim | solution.py:139
  (28 shorter events, 0.3 us)
Async XLA Ops:
  0.0 17.0 %copy-start = (bf16[3,3,3,512,16]{3,4,2,1,0:T(8,128)(2,1)S(1)}, bf16[3,3,3,512,16]{3,4,2,1,0:T(8,128)(2,1)}, u32[]{:S(2)}) copy-start(bf16[3,3,3,512,16]{3,4,2,1,0:T(8,128)(2,1)} %param.13) | copy-start | bytes 1327108
  0.0 16.8 %copy-start.5 = (bf16[1,1,2,4,64,512]{5,4,3,2,1,0:T(8,128)(2,1)S(1)}, bf16[1,1,2,4,64,512]{5,4,3,2,1,0:T(8,128)(2,1)}, u32[]{:S(2)}) copy-start(bf16[1,1,2,4,64,512]{5,4,3,2,1,0:T(8,128)(2,1)} %param.12) | copy-start | bytes 1572868
  1.1 14.6 %collective-permute-start.1 = (bf16[2,1,64,512]{3,2,1,0:T(8,128)(2,1)S(1)}, bf16[2,1,64,512]{3,2,1,0:T(8,128)(2,1)S(1)}, u32[]{:S(2)}, u32[]{:S(2)}) collective-permute-start(bf16[2,1,64,512]{3,2,1,0:T(8,128)(2,1)S(1)} %get-tuple-element.46), channel_id=1, source_target_pairs={{16,0},{17,1},{18,2},{19,3},{20,4},{21,5},{22,6},{23,7},{24,8},{25... | collective-permute-start | bytes 393224 | tf_op jit(solution)/shard_map/ppermute | solution.py:22
  2.4 13.3 %collective-permute-start = (bf16[2,1,64,512]{3,2,1,0:T(8,128)(2,1)S(1)}, bf16[2,1,64,512]{3,2,1,0:T(8,128)(2,1)S(1)}, u32[]{:S(2)}, u32[]{:S(2)}) collective-permute-start(bf16[2,1,64,512]{3,2,1,0:T(8,128)(2,1)S(1)} %get-tuple-element.45), channel_id=1, source_target_pairs={{0,16},{1,17},{2,18},{3,19},{4,20},{5,21},{6,22},{7,23},{8,24},{9,... | collective-permute-start | bytes 393224 | tf_op jit(solution)/shard_map/ppermute | solution.py:19
  21.6 1.5 %copy-start.9 = (f32[16]{0:T(128)S(1)}, f32[16]{0:T(128)}, u32[]{:S(2)}) copy-start(f32[16]{0:T(128)} %param.14) | copy-start | bytes 196
  36.3 1.8 %copy-start.8 = (bf16[64,4608]{1,0:T(8,128)(2,1)S(1)}, bf16[64,4608]{1,0:T(8,128)(2,1)}, u32[]{:S(2)}) copy-start(bf16[64,4608]{1,0:T(8,128)(2,1)} %param.15) | copy-start | bytes 1769476
  62.4 2.2 %copy-start.1 = (f32[2,128,12,128]{3,1,2,0:T(8,128)S(1)}, f32[2,128,12,128]{3,1,2,0:T(8,128)}, u32[]{:S(2)}) copy-start(f32[2,128,12,128]{3,1,2,0:T(8,128)} %copy.93) | copy-start | bytes 4718596
  62.4 2.2 %copy-start.10 = (f32[128]{0:T(128)S(1)}, f32[128]{0:T(128)}, u32[]{:S(2)}) copy-start(f32[128]{0:T(128)} %param.16) | copy-start | bytes 1540
  64.6 1.1 %copy-start.4 = (bf16[1,256,1536]{1,2,0:T(8,128)(2,1)S(1)}, bf16[1,256,1536]{1,2,0:T(8,128)(2,1)}, u32[]{:S(2)}) copy-start(bf16[1,256,1536]{1,2,0:T(8,128)(2,1)} %copy.100) | copy-start | bytes 2359300
  65.7 1.1 %copy-start.6 = (bf16[1,256,1536]{1,2,0:T(8,128)(2,1)S(1)}, bf16[1,256,1536]{1,2,0:T(8,128)(2,1)}, u32[]{:S(2)}) copy-start(bf16[1,256,1536]{1,2,0:T(8,128)(2,1)} %copy.99) | copy-start | bytes 2359300
  66.9 2.5 %copy-start.2 = (bf16[1,256,1536]{2,1,0:T(8,128)(2,1)S(1)}, bf16[1,256,1536]{2,1,0:T(8,128)(2,1)}, u32[]{:S(2)}) copy-start(bf16[1,256,1536]{2,1,0:T(8,128)(2,1)} %get-tuple-element.41) | copy-start | bytes 2359300
  68.1 2.4 %copy-start.3 = (bf16[1,256,1536]{2,1,0:T(8,128)(2,1)S(1)}, bf16[1,256,1536]{2,1,0:T(8,128)(2,1)}, u32[]{:S(2)}) copy-start(bf16[1,256,1536]{2,1,0:T(8,128)(2,1)} %get-tuple-element.43) | copy-start | bytes 2359300
  70.8 1.1 %copy-start.7 = (bf16[1,256,1536]{1,2,0:T(8,128)(2,1)S(1)}, bf16[1,256,1536]{1,2,0:T(8,128)(2,1)}, u32[]{:S(2)}) copy-start(bf16[1,256,1536]{1,2,0:T(8,128)(2,1)} %copy.90) | copy-start | bytes 2359300
where the time goes:
time: 74.5 us; the launch traced here: 73.9 us
  local copies, waits for them, and re-layouts  26 us (35%)
  other arithmetic  19.7 us (26%)
  blocking collectives  10.6 us (14%)
  matrix products  9.68 us (13%)
  starting transfers between devices  6.2 us (8%)
  between operations  1.7 us (2%)
    all_gather x1, blocking collectives, shards(): lax.all_gather(tokens[None], 'group', axis=0, tiled=True)  5.83 us
    mul x2, local copies, waits for them, and re-layouts, head_norm(): shaped * lax.rsqrt(jnp.mean(shaped * shaped, axis=-1, keepdims=True) + 1e...  5.46 us
    ppermute x1, starting transfers between devices, with_halo(): lax.ppermute(lax.slice_in_dim(block, block.shape[dim] - width, None, axis...  4.91 us
    all_gather x1, blocking collectives, shards(): flat_rows = lax.all_gather(slots, 'tile', axis=1, tiled=True)  4.76 us
    mul x1, other arithmetic, head_norm(): shaped * shaped  3.84 us
    dot_general x1, matrix products, shards(): jnp.einsum('ctf,fe->cte', flat_rows, pair_weight, preferred_element_type=...  3.66 us
    convert_element_type x1, other arithmetic, shards(): normed = head_norm(projected[..., :D], key_gain, HEAD).reshape(projected....  3.59 us
    mul x1, local copies, waits for them, and re-layouts, head_norm(): shaped * shaped  3.51 us
  transfers between devices with their start and end apart: 2, of which 0 were waited for; matrix products, arithmetic and copies ran while one was open for 10% of the time, Pallas kernels for 0%

commit v1 on v0

v1 whole, which is shorter than its diff:
```python
import functools
import math

import jax
import jax.numpy as jnp
from jax import lax
from jax.experimental import pallas as pl
from jax.experimental.pallas import tpu as pltpu
from jax.sharding import PartitionSpec as P

HEADS = 12
HEAD = 128
D = 1536
CAP = 2
EPS = 1e-06
BF16 = jnp.bfloat16
F32 = jnp.float32

VMEM = pl.BlockSpec(memory_space=pltpu.VMEM)
SMEM = pl.BlockSpec(memory_space=pltpu.SMEM)
HBM = pl.BlockSpec(memory_space=pltpu.HBM)


def in_vmem(*arrays):
    return [pltpu.with_memory_space_constraint(array, pltpu.VMEM) for array in arrays]


def column(row):
    size = row.shape[1]
    wide = jnp.broadcast_to(row, (size, size))
    down = lax.broadcasted_iota(jnp.int32, (size, size), 0)
    across = lax.broadcasted_iota(jnp.int32, (size, size), 1)
    return jnp.sum(jnp.where(down == across, wide, 0.0), axis=1, keepdims=True)


def conv_rows(features_ref, weight_ref, bias_ref, x_scr, w_scr, x_sem, w_sem, tiles):
    _, _, frames, rows, cols, _ = features_ref.shape
    lanes = frames * cols
    w_copy = pltpu.make_async_copy(weight_ref, w_scr, w_sem)
    w_copy.start()
    copies = []
    for row in range(rows):
        copy = pltpu.make_async_copy(features_ref.at[0, 0, :, row], x_scr.at[row], x_sem.at[row])
        copy.start()
        copies.append(copy)
    tile = lax.axis_index("tile")
    is_first = tile == 0
    is_last = tile == tiles - 1
    lane = lax.broadcasted_iota(jnp.int32, (16, lanes), 1)
    col = lane % cols
    in_first = lane < cols
    w_copy.wait()
    taps = []
    for pair in range(rows // 2):
        copies[2 * pair].wait()
        copies[2 * pair + 1].wait()
        block = x_scr[2 * pair : 2 * pair + 2].reshape(2 * lanes, -1)
        products = lax.dot_general(
            w_scr[...], block, (((1,), (1,)), ((), ())), preferred_element_type=F32
        )
        for half in range(2):
            part = products[:, half * lanes : (half + 1) * lanes]
            row_taps = []
            for b in range(3):
                row_taps.append([])
                for c in range(3):
                    tap = [part[(a * 9 + b * 3 + c) * 16 : (a * 9 + b * 3 + c + 1) * 16] for a in range(3)]
                    row_taps[b].append((tap[0] + tap[1], tap[2]))
            taps.append(row_taps)

    def finish(sums):
        def shifted(value, c):
            if c == 0:
                return jnp.where(col == 0, value, pltpu.roll(value, 1, 1))
            if c == 2:
                return jnp.where(col == cols - 1, value, pltpu.roll(value, lanes - 1, 1))
            return value

        early = sum(shifted(sums[c][0], c) for c in range(3))
        late = sum(shifted(sums[c][1], c) for c in range(3))
        return late + jnp.where(in_first, early, pltpu.roll(early, cols, 1))

    def add(*parts):
        return [tuple(sum(p[c][k] for p in parts) for k in range(2)) for c in range(3)]

    bias = column(bias_ref[...])
    out = []
    for row in range(rows):
        parts = [taps[row + b - 1][b] for b in range(3) if 0 <= row + b - 1 < rows]
        value = finish(add(*parts)) + bias
        if row == 0:
            value = value + jnp.where(is_first, finish(taps[0][0]), 0.0)
        if row == rows - 1:
            value = value + jnp.where(is_last, finish(taps[rows - 1][2]), 0.0)
        out.append(value)
    return out, finish(taps[rows - 1][0]), finish(taps[0][2]), is_first


def conv_pair_kernel(features_ref, weight_ref, bias_ref, send_ref, keep_ref, x_scr, w_scr, x_sem, w_sem):
    out, below, above, is_first = conv_rows(
        features_ref, weight_ref, bias_ref, x_scr, w_scr, x_sem, w_sem, 2
    )
    rows = len(out)
    for row in range(rows):
        send_ref[row] = out[row].astype(BF16)
    edge = jnp.where(is_first, out[rows - 1], out[0])
    owed = jnp.where(is_first, below, above)
    keep_ref[0] = edge
    keep_ref[1] = owed
    send_ref[rows] = (edge - edge.astype(BF16).astype(F32)).astype(BF16)
    high = owed.astype(BF16)
    send_ref[rows + 1] = high
    send_ref[rows + 2] = (owed - high.astype(F32)).astype(BF16)


def selection(lanes, cols):
    shape = (2 * lanes, 2 * lanes)
    src = lax.broadcasted_iota(jnp.int32, shape, 0)
    dst = lax.broadcasted_iota(jnp.int32, shape, 1)
    half = cols // 2
    x = dst // lanes
    f = dst % lanes // cols
    i = dst % cols // half
    j = dst % half
    want = i * lanes + f * cols + 2 * j + x
    return jnp.where(src == want, 1.0, 0.0).astype(BF16)


def to_tokens(latent_rows, cols):
    blocks = [
        jnp.concatenate([latent_rows[y], latent_rows[2 + y]], axis=1) for y in range(2)
    ]
    return jnp.concatenate(blocks, axis=0)


def finish_pair_kernel(send_ref, recv_ref, keep_ref, tokens_ref, *, cols):
    is_first = lax.axis_index("tile") == 0
    slots, zc, lanes = send_ref.shape
    rows = slots - 3
    mine = [send_ref[row].astype(F32) for row in range(rows)]
    theirs = [recv_ref[row].astype(F32) for row in range(rows)]
    my_edge = keep_ref[0] + (recv_ref[rows + 1].astype(F32) + recv_ref[rows + 2].astype(F32))
    their_edge = jnp.where(is_first, theirs[0], theirs[rows - 1]) + recv_ref[rows].astype(F32) + keep_ref[1]
    mine[0] = jnp.where(is_first, mine[0], my_edge)
    mine[rows - 1] = jnp.where(is_first, my_edge, mine[rows - 1])
    theirs[0] = jnp.where(is_first, their_edge, theirs[0])
    theirs[rows - 1] = jnp.where(is_first, theirs[rows - 1], their_edge)
    low = [jnp.where(is_first, a, b) for a, b in zip(mine, theirs)]
    high = [jnp.where(is_first, b, a) for a, b in zip(mine, theirs)]
    stacked = jnp.concatenate([to_tokens(low, cols), to_tokens(high, cols)], axis=0).astype(BF16)
    picked = jnp.dot(stacked, selection(lanes, cols), preferred_element_type=F32).astype(BF16)
    for t in range(2):
        for y in range(2):
            for x in range(2):
                tokens_ref[t, (2 * y + x) * zc : (2 * y + x + 1) * zc] = picked[
                    (2 * t + y) * zc : (2 * t + y + 1) * zc, x * lanes : (x + 1) * lanes
                ]


def conv_any_kernel(features_ref, weight_ref, bias_ref, part_ref, owed_ref, x_scr, w_scr, x_sem, w_sem, *, tiles):
    out, below, above, _ = conv_rows(
        features_ref, weight_ref, bias_ref, x_scr, w_scr, x_sem, w_sem, tiles
    )
    for row, value in enumerate(out):
        part_ref[row] = value
    owed_ref[0] = below
    owed_ref[1] = above


def finish_any_kernel(part_ref, from_low_ref, from_high_ref, tokens_ref, *, cols):
    rows, zc, lanes = part_ref.shape
    latent = [part_ref[row] for row in range(rows)]
    latent[0] = latent[0] + from_low_ref[...]
    latent[rows - 1] = latent[rows - 1] + from_high_ref[...]
    stacked = to_tokens(latent, cols).astype(BF16)
    picked = jnp.dot(stacked, selection(lanes, cols), preferred_element_type=F32).astype(BF16)
    for y in range(2):
        for x in range(2):
            tokens_ref[(2 * y + x) * zc : (2 * y + x + 1) * zc] = picked[
                y * zc : (y + 1) * zc, x * lanes : (x + 1) * lanes
            ]


def prepare_kernel(embed_ref, qgain_ref, kgain_ref, key_t_ref, qscale_ref, kscale_ref):
    key_t_ref[...] = jnp.transpose(embed_ref[:, D : 2 * D].astype(F32)).astype(BF16)
    qscale_ref[...] = qgain_ref[...] * (math.log2(math.e) / math.sqrt(HEAD))
    kscale_ref[...] = jnp.broadcast_to(column(kgain_ref[...]), kscale_ref.shape)


def attend_kernel(*refs, groups, sources, cols):
    bucket_ref, frames_ref = refs[:2]
    token_refs = refs[2 : 2 + sources]
    embed_ref, key_t_ref, qscale_ref, kscale_ref, out_ref = refs[2 + sources : 7 + sources]
    nat_scr, out_scr, sem = refs[7 + sources :]
    seq = lax.axis_index("seq")
    me = lax.axis_index("group")
    tile = lax.axis_index("tile")
    tiles, feat, lanes = token_refs[0].shape[-3:]
    clip = tiles * lanes
    src = [jnp.int32(0)] * CAP
    count = jnp.int32(0)
    for g in range(groups):
        hit = bucket_ref[seq, g] == me
        for slot in range(CAP):
            src[slot] = jnp.where(hit & (count == slot), g, src[slot])
        count = count + jnp.where(hit, 1, 0)

    query_gain = qscale_ref[...]
    key_gain = kscale_ref[...]
    frame_lane = lax.broadcasted_iota(jnp.int32, (1, lanes), 1) // cols
    frame_row = lax.broadcasted_iota(jnp.int32, (lanes, 1), 0) // cols
    copies = []
    for slot in range(CAP):
        filled = count > slot
        total = jnp.where(filled, frames_ref[seq, src[slot]], 0)
        if sources == 1:
            raw = token_refs[0][src[slot]].astype(F32)
        else:
            at = src[slot] ^ me
            raw = token_refs[0][...].astype(F32)
            for k in range(1, sources):
                raw = jnp.where(at == k, token_refs[k][...].astype(F32), raw)
        valid = jnp.where(frame_lane < total, 1.0, 0.0)
        counted = jnp.where(frame_lane < jnp.maximum(total, 1), 1.0, 0.0)
        row_keep = jnp.where(frame_row < total, 1.0, 0.0)
        tokens_t = jnp.concatenate([raw[t] * valid for t in range(tiles)], axis=1)
        nat_scr[slot] = jnp.transpose(tokens_t).astype(BF16)
        tokens_t = tokens_t.astype(BF16)
        natural = nat_scr[slot]
        mine = nat_scr[slot, pl.ds(pl.multiple_of(tile * lanes, lanes), lanes), :]
        for pair in range(HEADS // 2):
            span = slice(pair * 2 * HEAD, (pair + 1) * 2 * HEAD)
            keys = jnp.dot(key_t_ref[span, :], tokens_t, preferred_element_type=F32)
            queries = jnp.dot(mine, embed_ref[:, span], preferred_element_type=F32)
            values = jnp.dot(
                natural, embed_ref[:, 2 * D + span.start : 2 * D + span.stop], preferred_element_type=F32
            ).astype(BF16)
            for half in range(2):
                one = slice(half * HEAD, (half + 1) * HEAD)
                k = keys[one]
                k = k * lax.rsqrt(jnp.mean(k * k, axis=0, keepdims=True) + EPS) * key_gain
                q = queries[:, one]
                q = q * lax.rsqrt(jnp.mean(q * q, axis=1, keepdims=True) + EPS) * query_gain
                scores = jnp.dot(q.astype(BF16), k.astype(BF16), preferred_element_type=F32)
                weights = jnp.exp2(scores)
                folded = weights[:, :lanes]
                for t in range(1, tiles):
                    folded = folded + weights[:, t * lanes : (t + 1) * lanes]
                totals = jnp.sum(folded * counted, axis=1, keepdims=True)
                mixed = jnp.dot(weights.astype(BF16), values[:, one], preferred_element_type=F32)
                head = 2 * pair + half
                out_scr[slot, :, head * HEAD : (head + 1) * HEAD] = (
                    mixed * (row_keep / totals)
                ).astype(BF16)
        copy = pltpu.make_async_copy(out_scr.at[slot], out_ref.at[slot], sem.at[slot])
        copy.start()
        copies.append(copy)
    for copy in copies:
        copy.wait()


def clip_tokens(features, weight_t, bias_row):
    _, _, frames, rows, cols, channels = features.shape
    zc = bias_row.shape[1]
    lanes = frames * cols
    tiles = lax.axis_size("tile")
    scratch = [
        pltpu.VMEM((rows, frames, cols, channels), BF16),
        pltpu.VMEM(weight_t.shape, BF16),
        pltpu.SemaphoreType.DMA((rows,)),
        pltpu.SemaphoreType.DMA,
    ]
    if tiles == 2:
        send, keep = pl.pallas_call(
            conv_pair_kernel,
            out_shape=(pltpu.VMEM((rows + 3, zc, lanes), BF16), pltpu.VMEM((2, zc, lanes), F32)),
            in_specs=[HBM, HBM, VMEM],
            out_specs=(VMEM, VMEM),
            scratch_shapes=scratch,
            name="conv",
        )(features, weight_t, bias_row)
        recv = lax.ppermute(send, "tile", [(0, 1), (1, 0)])
        return pl.pallas_call(
            functools.partial(finish_pair_kernel, cols=cols),
            out_shape=pltpu.VMEM((2, 4 * zc, lanes), BF16),
            in_specs=[VMEM, VMEM, VMEM],
            out_specs=VMEM,
            name="finish",
        )(*in_vmem(send, recv, keep))
    part, owed = pl.pallas_call(
        functools.partial(conv_any_kernel, tiles=tiles),
        out_shape=(pltpu.VMEM((rows, zc, lanes), F32), pltpu.VMEM((2, zc, lanes), F32)),
        in_specs=[HBM, HBM, VMEM],
        out_specs=(VMEM, VMEM),
        scratch_shapes=scratch,
        name="conv",
    )(features, weight_t, bias_row)
    up = [(i, i + 1) for i in range(tiles - 1)]
    from_low = lax.ppermute(owed[0], "tile", up)
    from_high = lax.ppermute(owed[1], "tile", [(b, a) for a, b in up])
    tokens = pl.pallas_call(
        functools.partial(finish_any_kernel, cols=cols),
        out_shape=pltpu.VMEM((4 * zc, lanes), BF16),
        in_specs=[VMEM, VMEM, VMEM],
        out_specs=VMEM,
        name="finish",
    )(*in_vmem(part, from_low, from_high))
    return lax.all_gather(tokens, "tile", axis=0)


def shards(features, conv_weight, conv_bias, embed_qkv, query_gain, key_gain, bucket, frames):
    _, _, frame_count, rows, cols, channels = features.shape
    zc = conv_weight.shape[-1]
    lanes = frame_count * cols
    tiles = lax.axis_size("tile")
    groups = lax.axis_size("group")
    weight_t = jnp.transpose(conv_weight, (0, 1, 2, 4, 3)).reshape(-1, channels)
    tokens = clip_tokens(features, weight_t, conv_bias.reshape(1, -1))
    (embed,) = in_vmem(embed_qkv)
    key_t, query_scale, key_scale = pl.pallas_call(
        prepare_kernel,
        out_shape=(
            pltpu.VMEM((D, 4 * zc), BF16),
            pltpu.VMEM((1, HEAD), F32),
            pltpu.VMEM((HEAD, tiles * lanes), F32),
        ),
        in_specs=[VMEM, VMEM, VMEM],
        out_specs=(VMEM, VMEM, VMEM),
        name="prepare",
    )(embed, query_gain.reshape(1, -1), key_gain.reshape(1, -1))
    if groups in (2, 4):
        sources = [tokens] + [
            lax.ppermute(tokens, "group", [(i, i ^ k) for i in range(groups)]) for k in range(1, groups)
        ]
    else:
        sources = [lax.all_gather(tokens, "group", axis=0)]
    out = pl.pallas_call(
        functools.partial(attend_kernel, groups=groups, sources=len(sources), cols=cols),
        out_shape=jax.ShapeDtypeStruct((CAP, lanes, D), BF16),
        in_specs=[SMEM, SMEM] + [VMEM] * (len(sources) + 4),
        out_specs=HBM,
        scratch_shapes=[
            pltpu.VMEM((CAP, tiles * lanes, 4 * zc), BF16),
            pltpu.VMEM((CAP, lanes, D), BF16),
            pltpu.SemaphoreType.DMA((CAP,)),
        ],
        name="attend",
    )(bucket, frames, *in_vmem(*sources, embed, key_t, query_scale, key_scale))
    return out[None, None]


def solution(mesh):
    in_specs = (P("seq", "group", None, "tile", None, None), P(), P(), P(), P(), P(), P(), P())
    out_specs = P("seq", "group", None, "tile", None)
    return jax.shard_map(shards, mesh=mesh, in_specs=in_specs, out_specs=out_specs, check_vma=False)
```

time: 74.5 us -> 19.1 us (0.26)
  the two profiles are of different devices: /device:TPU:0 before, /device:TPU:1 now
where the time goes in v1:
time: 19.1 us; the launch traced here: 18.9 us
  Pallas kernels  10.5 us (55%)
  starting transfers between devices  5.74 us (30%)
  waiting for transfers between devices  2.67 us (14%)
    pallas_call x1, Pallas kernels, shards(): pl.pallas_call(functools.partial(attend_kernel, groups=groups, sources=le...  6.53 us
    ppermute x3, starting transfers between devices, shards(): lax.ppermute(tokens, 'group', [(i, i ^ k) for i in range(groups)])  3.62 us
    pallas_call x1, Pallas kernels, clip_tokens(): pl.pallas_call(conv_pair_kernel, out_shape=(pltpu.VMEM((rows + 3, zc, lan...  2.9 us
    ppermute x1, starting transfers between devices, clip_tokens(): recv = lax.ppermute(send, 'tile', [(0, 1), (1, 0)])  2.12 us
    ppermute x3, waiting for transfers between devices, shards(): lax.ppermute(tokens, 'group', [(i, i ^ k) for i in range(groups)])  1.41 us
    ppermute x1, waiting for transfers between devices, clip_tokens(): recv = lax.ppermute(send, 'tile', [(0, 1), (1, 0)])  1.26 us
    pallas_call x1, Pallas kernels, shards(): pl.pallas_call(prepare_kernel, out_shape=(pltpu.VMEM((D, 4 * zc), BF16),...  0.88 us
  transfers between devices with their start and end apart: 4, of which 3 were waited for; matrix products, arithmetic and copies ran while one was open for 0% of the time, Pallas kernels for 5%

profile of v1, /device:TPU:1, one launch (start us, length us, event | category | flops | bytes accessed | tf_op | source)
XLA Modules:
  0.0 18.9 jit_solution(15860117543110383956)
XLA Ops:
  0.0 0.0 copy-start
  0.0 2.9 %conv.1 = (bf16[7,16,128]{2,1,0:T(8,128)(2,1)S(1)}, f32[2,16,128]{2,1,0:T(8,128)S(1)}) custom-call(bf16[1,1,2,4,64,512]{5,4,3,2,1,0:T(8,128)(2,1)} %features_ref.1, bf16[432,512]{1,0:T(8,128)(2,1)} %bitcast.7, f32[1,16]{1,0:T(1,128)} %bitcast.8), custom_call_target="tpu_custom_call" | custom-call | tf_op jit(solution)/shard_map/conv/pallas_call | solution.py:274
  2.9 2.1 %collective-permute-start = (bf16[7,16,128]{2,1,0:T(8,128)(2,1)S(1)}, bf16[7,16,128]{2,1,0:T(8,128)(2,1)S(1)}, u32[]{:S(2)}, u32[]{:S(2)}) collective-permute-start(bf16[7,16,128]{2,1,0:T(8,128)(2,1)S(1)} %get-tuple-element.10.send_ref), channel_id=1, source_target_pairs={{0,16},{16,0},{1,17},{17,1},{2,18},{18,2},{3,19},{19,3},{4,20},{20... | collective-permute-start | bytes 86024 | tf_op jit(solution)/shard_map/ppermute | solution.py:282
  5.0 1.3 %collective-permute-done.recv_ref = bf16[7,16,128]{2,1,0:T(8,128)(2,1)S(1)} collective-permute-done((bf16[7,16,128]{2,1,0:T(8,128)(2,1)S(1)}, bf16[7,16,128]{2,1,0:T(8,128)(2,1)S(1)}, u32[]{:S(2)}, u32[]{:S(2)}) %collective-permute-start) | collective-permute-done | bytes 28704 | tf_op jit(solution)/shard_map/ppermute | solution.py:282
  6.3 0.2 finish.1.refs_2_
  6.5 3.2 %collective-permute-start.3 = (bf16[2,64,128]{2,1,0:T(8,128)(2,1)S(1)}, bf16[2,64,128]{2,1,0:T(8,128)(2,1)S(1)}, u32[]{:S(2)}, u32[]{:S(2)}) collective-permute-start(bf16[2,64,128]{2,1,0:T(8,128)(2,1)S(1)} %finish.1.refs_2_), channel_id=1, source_target_pairs={{0,3},{1,2},{2,1},{3,0},{4,7},{5,6},{6,5},{7,4},{8,11},{9,10},{10,... | collective-permute-start | bytes 98312 | tf_op jit(solution)/shard_map/ppermute | solution.py:333
  9.6 0.0 collective-permute-start.2
  9.6 0.5 %collective-permute-start.1 = (bf16[2,64,128]{2,1,0:T(8,128)(2,1)S(1)}, bf16[2,64,128]{2,1,0:T(8,128)(2,1)S(1)}, u32[]{:S(2)}, u32[]{:S(2)}) collective-permute-start(bf16[2,64,128]{2,1,0:T(8,128)(2,1)S(1)} %finish.1.refs_2_), channel_id=1, source_target_pairs={{0,1},{1,0},{2,3},{3,2},{4,5},{5,4},{6,7},{7,6},{8,9},{9,8},{10,11... | collective-permute-start | bytes 98312 | tf_op jit(solution)/shard_map/ppermute | solution.py:333
  10.1 0.0 copy-done
  10.1 0.9 %prepare.1 = (bf16[1536,64]{1,0:T(8,128)(2,1)S(1)}, f32[1,128]{1,0:T(1,128)S(1)}, f32[128,256]{1,0:T(8,128)S(1)}) custom-call(bf16[64,4608]{1,0:T(8,128)(2,1)S(1)} %copy-done, f32[1,128]{1,0:T(1,128)} %bitcast.9, f32[1,128]{1,0:T(1,128)} %bitcast.10), custom_call_target="tpu_custom_call" | custom-call | tf_op jit(solution)/shard_map/prepare/pallas_call | solution.py:320
  11.0 0.2 %collective-permute-done.3.refs_5_ = bf16[2,64,128]{2,1,0:T(8,128)(2,1)S(1)} collective-permute-done((bf16[2,64,128]{2,1,0:T(8,128)(2,1)S(1)}, bf16[2,64,128]{2,1,0:T(8,128)(2,1)S(1)}, u32[]{:S(2)}, u32[]{:S(2)}) %collective-permute-start.3) | collective-permute-done | bytes 32800 | tf_op jit(solution)/shard_map/ppermute | solution.py:333
  11.2 1.2 %collective-permute-done.2.refs_4_ = bf16[2,64,128]{2,1,0:T(8,128)(2,1)S(1)} collective-permute-done((bf16[2,64,128]{2,1,0:T(8,128)(2,1)S(1)}, bf16[2,64,128]{2,1,0:T(8,128)(2,1)S(1)}, u32[]{:S(2)}, u32[]{:S(2)}) %collective-permute-start.2) | collective-permute-done | bytes 32800 | tf_op jit(solution)/shard_map/ppermute | solution.py:333
  12.4 0.0 collective-permute-done.1.refs_3_
  12.4 6.5 %attend.1 = bf16[2,128,1536]{2,1,0:T(8,128)(2,1)} custom-call(s32[4,4]{1,0:T(4,128)} %refs_0_.1, s32[4,4]{1,0:T(4,128)} %refs_1_.1, bf16[2,64,128]{2,1,0:T(8,128)(2,1)S(1)} %finish.1.refs_2_, bf16[2,64,128]{2,1,0:T(8,128)(2,1)S(1)} %collective-permute-done.1.refs_3_, bf16[2,64,128]{2,1,0:T(8,128)(2,1)S(1)} %collective-permute-done.2.refs_4_, ...), custom_call_target="tpu_custom_call" | custom-call | tf_op jit(solution)/shard_map/attend/pallas_call | solution.py:337
Async XLA Ops:
  0.0 10.1 %copy-start = (bf16[64,4608]{1,0:T(8,128)(2,1)S(1)}, bf16[64,4608]{1,0:T(8,128)(2,1)}, u32[]{:S(2)}) copy-start(bf16[64,4608]{1,0:T(8,128)(2,1)} %refs_6_.1) | copy-start | bytes 1769476
  2.9 3.4 %collective-permute-start = (bf16[7,16,128]{2,1,0:T(8,128)(2,1)S(1)}, bf16[7,16,128]{2,1,0:T(8,128)(2,1)S(1)}, u32[]{:S(2)}, u32[]{:S(2)}) collective-permute-start(bf16[7,16,128]{2,1,0:T(8,128)(2,1)S(1)} %get-tuple-element.10.send_ref), channel_id=1, source_target_pairs={{0,16},{16,0},{1,17},{17,1},{2,18},{18,2},{3,19},{19,3},{4,20},{20... | collective-permute-start | bytes 86024 | tf_op jit(solution)/shard_map/ppermute | solution.py:282
  6.5 4.7 %collective-permute-start.3 = (bf16[2,64,128]{2,1,0:T(8,128)(2,1)S(1)}, bf16[2,64,128]{2,1,0:T(8,128)(2,1)S(1)}, u32[]{:S(2)}, u32[]{:S(2)}) collective-permute-start(bf16[2,64,128]{2,1,0:T(8,128)(2,1)S(1)} %finish.1.refs_2_), channel_id=1, source_target_pairs={{0,3},{1,2},{2,1},{3,0},{4,7},{5,6},{6,5},{7,4},{8,11},{9,10},{10,... | collective-permute-start | bytes 98312 | tf_op jit(solution)/shard_map/ppermute | solution.py:333
  9.6 2.8 %collective-permute-start.2 = (bf16[2,64,128]{2,1,0:T(8,128)(2,1)S(1)}, bf16[2,64,128]{2,1,0:T(8,128)(2,1)S(1)}, u32[]{:S(2)}, u32[]{:S(2)}) collective-permute-start(bf16[2,64,128]{2,1,0:T(8,128)(2,1)S(1)} %finish.1.refs_2_), channel_id=1, source_target_pairs={{0,2},{1,3},{2,0},{3,1},{4,6},{5,7},{6,4},{7,5},{8,10},{9,11},{10,... | collective-permute-start | bytes 98312 | tf_op jit(solution)/shard_map/ppermute | solution.py:333
  9.6 2.8 %collective-permute-start.1 = (bf16[2,64,128]{2,1,0:T(8,128)(2,1)S(1)}, bf16[2,64,128]{2,1,0:T(8,128)(2,1)S(1)}, u32[]{:S(2)}, u32[]{:S(2)}) collective-permute-start(bf16[2,64,128]{2,1,0:T(8,128)(2,1)S(1)} %finish.1.refs_2_), channel_id=1, source_target_pairs={{0,1},{1,0},{2,3},{3,2},{4,5},{5,4},{6,7},{7,6},{8,9},{9,8},{10,11... | collective-permute-start | bytes 98312 | tf_op jit(solution)/shard_map/ppermute | solution.py:333

commit v2 on v1

--- a/solution.py
+++ b/solution.py
@@ -33,7 +33,7 @@
     return jnp.sum(jnp.where(down == across, wide, 0.0), axis=1, keepdims=True)
 
 
-def conv_rows(features_ref, weight_ref, bias_ref, x_scr, w_scr, x_sem, w_sem, tiles):
+def conv_rows(features_ref, weight_ref, bias_ref, x_scr, w_scr, b_scr, x_sem, w_sem, b_sem, tiles):
     _, _, frames, rows, cols, _ = features_ref.shape
     lanes = frames * cols
     w_copy = pltpu.make_async_copy(weight_ref, w_scr, w_sem)
@@ -43,12 +43,16 @@
         copy = pltpu.make_async_copy(features_ref.at[0, 0, :, row], x_scr.at[row], x_sem.at[row])
         copy.start()
         copies.append(copy)
+    b_copy = pltpu.make_async_copy(bias_ref, b_scr, b_sem)
+    b_copy.start()
     tile = lax.axis_index("tile")
     is_first = tile == 0
     is_last = tile == tiles - 1
     lane = lax.broadcasted_iota(jnp.int32, (16, lanes), 1)
     col = lane % cols
     in_first = lane < cols
+    b_copy.wait()
+    bias = column(b_scr[...])
     w_copy.wait()
     taps = []
     for pair in range(rows // 2):
@@ -83,7 +87,6 @@
     def add(*parts):
         return [tuple(sum(p[c][k] for p in parts) for k in range(2)) for c in range(3)]
 
-    bias = column(bias_ref[...])
     out = []
     for row in range(rows):
         parts = [taps[row + b - 1][b] for b in range(3) if 0 <= row + b - 1 < rows]
@@ -96,10 +99,8 @@
     return out, finish(taps[rows - 1][0]), finish(taps[0][2]), is_first
 
 
-def conv_pair_kernel(features_ref, weight_ref, bias_ref, send_ref, keep_ref, x_scr, w_scr, x_sem, w_sem):
-    out, below, above, is_first = conv_rows(
-        features_ref, weight_ref, bias_ref, x_scr, w_scr, x_sem, w_sem, 2
-    )
+def conv_pair_kernel(features_ref, weight_ref, bias_ref, send_ref, keep_ref, *scratch):
+    out, below, above, is_first = conv_rows(features_ref, weight_ref, bias_ref, *scratch, 2)
     rows = len(out)
     for row in range(rows):
         send_ref[row] = out[row].astype(BF16)
@@ -157,10 +158,8 @@
                 ]
 
 
-def conv_any_kernel(features_ref, weight_ref, bias_ref, part_ref, owed_ref, x_scr, w_scr, x_sem, w_sem, *, tiles):
-    out, below, above, _ = conv_rows(
-        features_ref, weight_ref, bias_ref, x_scr, w_scr, x_sem, w_sem, tiles
-    )
+def conv_any_kernel(features_ref, weight_ref, bias_ref, part_ref, owed_ref, *scratch, tiles):
+    out, below, above, _ = conv_rows(features_ref, weight_ref, bias_ref, *scratch, tiles)
     for row, value in enumerate(out):
         part_ref[row] = value
     owed_ref[0] = below
@@ -181,80 +180,106 @@
             ]
 
 
-def prepare_kernel(embed_ref, qgain_ref, kgain_ref, key_t_ref, qscale_ref, kscale_ref):
-    key_t_ref[...] = jnp.transpose(embed_ref[:, D : 2 * D].astype(F32)).astype(BF16)
-    qscale_ref[...] = qgain_ref[...] * (math.log2(math.e) / math.sqrt(HEAD))
-    kscale_ref[...] = jnp.broadcast_to(column(kgain_ref[...]), kscale_ref.shape)
-
-
-def attend_kernel(*refs, groups, sources, cols):
-    bucket_ref, frames_ref = refs[:2]
-    token_refs = refs[2 : 2 + sources]
-    embed_ref, key_t_ref, qscale_ref, kscale_ref, out_ref = refs[2 + sources : 7 + sources]
-    nat_scr, out_scr, sem = refs[7 + sources :]
+def prepare_kernel(bucket_ref, frames_ref, embed_ref, qgain_ref, kgain_ref, slot_ref, key_t_ref, qscale_ref, kscale_ref):
     seq = lax.axis_index("seq")
     me = lax.axis_index("group")
-    tile = lax.axis_index("tile")
-    tiles, feat, lanes = token_refs[0].shape[-3:]
-    clip = tiles * lanes
     src = [jnp.int32(0)] * CAP
     count = jnp.int32(0)
-    for g in range(groups):
+    for g in range(bucket_ref.shape[1]):
         hit = bucket_ref[seq, g] == me
         for slot in range(CAP):
             src[slot] = jnp.where(hit & (count == slot), g, src[slot])
         count = count + jnp.where(hit, 1, 0)
-
-    query_gain = qscale_ref[...]
-    key_gain = kscale_ref[...]
+    for slot in range(CAP):
+        slot_ref[0, slot] = src[slot]
+        slot_ref[1, slot] = jnp.where(count > slot, frames_ref[seq, src[slot]], 0)
+    key_t_ref[...] = jnp.transpose(embed_ref[:, D : 2 * D].astype(F32)).astype(BF16)
+    qscale_ref[...] = qgain_ref[...] * math.log2(math.e)
+    kscale_ref[...] = jnp.broadcast_to(column(kgain_ref[...]) * math.sqrt(HEAD), kscale_ref.shape)
+
+
+def attend_kernel(slot_ref, *refs, sources, cols):
+    token_refs = refs[:sources]
+    embed_ref, key_t_ref, qscale_ref, kscale_ref, out_ref = refs[sources : 5 + sources]
+    nat_scr, tr_scr, k_scr, q_scr, v_scr, p_scr, r_scr, out_scr, sem = refs[5 + sources :]
+    me = lax.axis_index("group")
+    tile = lax.axis_index("tile")
+    tiles, _, lanes = token_refs[0].shape[-3:]
     frame_lane = lax.broadcasted_iota(jnp.int32, (1, lanes), 1) // cols
     frame_row = lax.broadcasted_iota(jnp.int32, (lanes, 1), 0) // cols
-    copies = []
+    counted, row_keep = [], []
     for slot in range(CAP):
-        filled = count > slot
-        total = jnp.where(filled, frames_ref[seq, src[slot]], 0)
+        source = slot_ref[0, slot]
+        total = slot_ref[1, slot]
         if sources == 1:
-            raw = token_refs[0][src[slot]].astype(F32)
+            raw = token_refs[0][source].astype(F32)
         else:
-            at = src[slot] ^ me
             raw = token_refs[0][...].astype(F32)
             for k in range(1, sources):
-                raw = jnp.where(at == k, token_refs[k][...].astype(F32), raw)
+                raw = jnp.where((source ^ me) == k, token_refs[k][...].astype(F32), raw)
         valid = jnp.where(frame_lane < total, 1.0, 0.0)
-        counted = jnp.where(frame_lane < jnp.maximum(total, 1), 1.0, 0.0)
-        row_keep = jnp.where(frame_row < total, 1.0, 0.0)
+        counted.append(jnp.where(frame_lane < jnp.maximum(total, 1), 1.0, 0.0))
+        row_keep.append(jnp.where(frame_row < total, 1.0, 0.0))
         tokens_t = jnp.concatenate([raw[t] * valid for t in range(tiles)], axis=1)
         nat_scr[slot] = jnp.transpose(tokens_t).astype(BF16)
-        tokens_t = tokens_t.astype(BF16)
-        natural = nat_scr[slot]
+        tr_scr[slot] = tokens_t.astype(BF16)
+
+    pairs = HEADS // 2
+    steps = CAP * pairs
+
+    def project(step):
+        slot, pair = divmod(step, pairs)
+        span = slice(pair * 2 * HEAD, (pair + 1) * 2 * HEAD)
         mine = nat_scr[slot, pl.ds(pl.multiple_of(tile * lanes, lanes), lanes), :]
-        for pair in range(HEADS // 2):
-            span = slice(pair * 2 * HEAD, (pair + 1) * 2 * HEAD)
-            keys = jnp.dot(key_t_ref[span, :], tokens_t, preferred_element_type=F32)
-            queries = jnp.dot(mine, embed_ref[:, span], preferred_element_type=F32)
-            values = jnp.dot(
-                natural, embed_ref[:, 2 * D + span.start : 2 * D + span.stop], preferred_element_type=F32
-            ).astype(BF16)
-            for half in range(2):
-                one = slice(half * HEAD, (half + 1) * HEAD)
-                k = keys[one]
-                k = k * lax.rsqrt(jnp.mean(k * k, axis=0, keepdims=True) + EPS) * key_gain
-                q = queries[:, one]
-                q = q * lax.rsqrt(jnp.mean(q * q, axis=1, keepdims=True) + EPS) * query_gain
-                scores = jnp.dot(q.astype(BF16), k.astype(BF16), preferred_element_type=F32)
-                weights = jnp.exp2(scores)
-                folded = weights[:, :lanes]
-                for t in range(1, tiles):
-                    folded = folded + weights[:, t * lanes : (t + 1) * lanes]
-                totals = jnp.sum(folded * counted, axis=1, keepdims=True)
-                mixed = jnp.dot(weights.astype(BF16), values[:, one], preferred_element_type=F32)
-                head = 2 * pair + half
-                out_scr[slot, :, head * HEAD : (head + 1) * HEAD] = (
-                    mixed * (row_keep / totals)
-                ).astype(BF16)
-        copy = pltpu.make_async_copy(out_scr.at[slot], out_ref.at[slot], sem.at[slot])
-        copy.start()
-        copies.append(copy)
+        queries = jnp.dot(mine, embed_ref[:, span], preferred_element_type=F32)
+        for half in range(2):
+            one = slice(half * HEAD, (half + 1) * HEAD)
+            k = jnp.dot(
+                key_t_ref[span.start + one.start : span.start + one.stop, :],
+                tr_scr[slot],
+                preferred_element_type=F32,
+            )
+            k = k * lax.rsqrt(jnp.sum(k * k, axis=0, keepdims=True) + HEAD * EPS) * kscale_ref[...]
+            k_scr[step % 2, half] = k.astype(BF16)
+            q = queries[:, one]
+            q = q * lax.rsqrt(jnp.sum(q * q, axis=1, keepdims=True) + HEAD * EPS) * qscale_ref[...]
+            q_scr[step % 2, half] = q.astype(BF16)
+        v_scr[step % 3] = jnp.dot(
+            nat_scr[slot], embed_ref[:, 2 * D + span.start : 2 * D + span.stop], preferred_element_type=F32
+        ).astype(BF16)
+
+    def score(step):
+        slot = step // pairs
+        for half in range(2):
+            scores = jnp.dot(q_scr[step % 2, half], k_scr[step % 2, half], preferred_element_type=F32)
+            weights = jnp.exp2(scores)
+            p_scr[step % 2, half] = weights.astype(BF16)
+            folded = weights[:, :lanes]
+            for t in range(1, tiles):
+                folded = folded + weights[:, t * lanes : (t + 1) * lanes]
+            totals = jnp.sum(folded * counted[slot], axis=1, keepdims=True)
+            r_scr[step % 2, half] = row_keep[slot] / totals
+
+    def mix(step):
+        slot, pair = divmod(step, pairs)
+        for half in range(2):
+            one = slice(half * HEAD, (half + 1) * HEAD)
+            mixed = jnp.dot(p_scr[step % 2, half], v_scr[step % 3, :, one], preferred_element_type=F32)
+            start = pair * 2 * HEAD + one.start
+            out_scr[slot, :, start : start + HEAD] = (mixed * r_scr[step % 2, half]).astype(BF16)
+
+    copies = []
+    for step in range(steps + 2):
+        if step >= 2:
+            mix(step - 2)
+            if (step - 1) % pairs == 0:
+                slot = (step - 2) // pairs
+                copies.append(pltpu.make_async_copy(out_scr.at[slot], out_ref.at[slot], sem.at[slot]))
+                copies[-1].start()
+        if 1 <= step <= steps:
+            score(step - 1)
+        if step < steps:
+            project(step)
     for copy in copies:
         copy.wait()
 
@@ -267,14 +292,16 @@
     scratch = [
         pltpu.VMEM((rows, frames, cols, channels), BF16),
         pltpu.VMEM(weight_t.shape, BF16),
+        pltpu.VMEM(bias_row.shape, F32),
         pltpu.SemaphoreType.DMA((rows,)),
+        pltpu.SemaphoreType.DMA,
         pltpu.SemaphoreType.DMA,
     ]
     if tiles == 2:
         send, keep = pl.pallas_call(
             conv_pair_kernel,
             out_shape=(pltpu.VMEM((rows + 3, zc, lanes), BF16), pltpu.VMEM((2, zc, lanes), F32)),
-            in_specs=[HBM, HBM, VMEM],
+            in_specs=[HBM, HBM, HBM],
             out_specs=(VMEM, VMEM),
             scratch_shapes=scratch,
             name="conv",
@@ -290,7 +317,7 @@
     part, owed = pl.pallas_call(
         functools.partial(conv_any_kernel, tiles=tiles),
         out_shape=(pltpu.VMEM((rows, zc, lanes), F32), pltpu.VMEM((2, zc, lanes), F32)),
-        in_specs=[HBM, HBM, VMEM],
+        in_specs=[HBM, HBM, HBM],
         out_specs=(VMEM, VMEM),
         scratch_shapes=scratch,
         name="conv",
@@ -317,35 +344,43 @@
     weight_t = jnp.transpose(conv_weight, (0, 1, 2, 4, 3)).reshape(-1, channels)
     tokens = clip_tokens(features, weight_t, conv_bias.reshape(1, -1))
     (embed,) = in_vmem(embed_qkv)
-    key_t, query_scale, key_scale = pl.pallas_call(
+    slots, key_t, query_scale, key_scale = pl.pallas_call(
         prepare_kernel,
         out_shape=(
+            pltpu.SMEM((2, CAP), jnp.int32),
             pltpu.VMEM((D, 4 * zc), BF16),
             pltpu.VMEM((1, HEAD), F32),
             pltpu.VMEM((HEAD, tiles * lanes), F32),
         ),
-        in_specs=[VMEM, VMEM, VMEM],
-        out_specs=(VMEM, VMEM, VMEM),
+        in_specs=[SMEM, SMEM, VMEM, VMEM, VMEM],
+        out_specs=(SMEM, VMEM, VMEM, VMEM),
         name="prepare",
-    )(embed, query_gain.reshape(1, -1), key_gain.reshape(1, -1))
+    )(bucket, frames, embed, query_gain.reshape(1, -1), key_gain.reshape(1, -1))
     if groups in (2, 4):
         sources = [tokens] + [
             lax.ppermute(tokens, "group", [(i, i ^ k) for i in range(groups)]) for k in range(1, groups)
         ]
     else:
         sources = [lax.all_gather(tokens, "group", axis=0)]
+    clip = tiles * lanes
     out = pl.pallas_call(
-        functools.partial(attend_kernel, groups=groups, sources=len(sources), cols=cols),
+        functools.partial(attend_kernel, sources=len(sources), cols=cols),
         out_shape=jax.ShapeDtypeStruct((CAP, lanes, D), BF16),
-        in_specs=[SMEM, SMEM] + [VMEM] * (len(sources) + 4),
+        in_specs=[SMEM] + [VMEM] * (len(sources) + 4),
         out_specs=HBM,
         scratch_shapes=[
-            pltpu.VMEM((CAP, tiles * lanes, 4 * zc), BF16),
+            pltpu.VMEM((CAP, clip, 4 * zc), BF16),
+            pltpu.VMEM((CAP, 4 * zc, clip), BF16),
+            pltpu.VMEM((2, 2, HEAD, clip), BF16),
+            pltpu.VMEM((2, 2, lanes, HEAD), BF16),
+            pltpu.VMEM((3, clip, 2 * HEAD), BF16),
+            pltpu.VMEM((2, 2, lanes, clip), BF16),
+            pltpu.VMEM((2, 2, lanes, 1), F32),
             pltpu.VMEM((CAP, lanes, D), BF16),
             pltpu.SemaphoreType.DMA((CAP,)),
         ],
         name="attend",
-    )(bucket, frames, *in_vmem(*sources, embed, key_t, query_scale, key_scale))
+    )(pltpu.with_memory_space_constraint(slots, pltpu.SMEM), *in_vmem(*sources, embed, key_t, query_scale, key_scale))
     return out[None, None]
 
 

time: 19.1 us -> 16.6 us (0.87)
  Pallas kernels: 10.5 us -> 8.01 us
    pallas_call x2, Pallas kernels: 7.41 us -> 5.61 us  [the longest x1 4.67 us: shards(): pl.pallas_call(functools.partial(attend_kernel, sources=len(sources), col...]
    pallas_call x1, Pallas kernels: 2.9 us -> 2.25 us  [clip_tokens(): pl.pallas_call(conv_pair_kernel, out_shape=(pltpu.VMEM((rows + 3, zc, lan...]
  transfers between devices with their start and end apart: 4 -> 4, of which waited for: 3 -> 3; matrix products, arithmetic and copies ran while one was open for 0% -> 0% of each run, Pallas kernels for 5% -> 6%
where the time goes in v2:
time: 16.6 us; the launch traced here: 16.4 us
  Pallas kernels  8.01 us (48%)
  starting transfers between devices  5.74 us (35%)
  waiting for transfers between devices  2.61 us (16%)
    pallas_call x1, Pallas kernels, shards(): pl.pallas_call(functools.partial(attend_kernel, sources=len(sources), col...  4.67 us
    ppermute x3, starting transfers between devices, shards(): lax.ppermute(tokens, 'group', [(i, i ^ k) for i in range(groups)])  3.61 us
    pallas_call x1, Pallas kernels, clip_tokens(): pl.pallas_call(conv_pair_kernel, out_shape=(pltpu.VMEM((rows + 3, zc, lan...  2.25 us
    ppermute x1, starting transfers between devices, clip_tokens(): recv = lax.ppermute(send, 'tile', [(0, 1), (1, 0)])  2.12 us
    ppermute x3, waiting for transfers between devices, shards(): lax.ppermute(tokens, 'group', [(i, i ^ k) for i in range(groups)])  1.35 us
    ppermute x1, waiting for transfers between devices, clip_tokens(): recv = lax.ppermute(send, 'tile', [(0, 1), (1, 0)])  1.26 us
    pallas_call x1, Pallas kernels, shards(): pl.pallas_call(prepare_kernel, out_shape=(pltpu.SMEM((2, CAP), jnp.int32)...  0.94 us
  transfers between devices with their start and end apart: 4, of which 3 were waited for; matrix products, arithmetic and copies ran while one was open for 0% of the time, Pallas kernels for 6%

profile of v2, /device:TPU:1, one launch (start us, length us, event | category | flops | bytes accessed | tf_op | source)
XLA Modules:
  0.0 16.4 jit_solution(17695776787039706697)
XLA Ops:
  0.0 0.0 copy-start
  0.0 2.2 %conv.1 = (bf16[7,16,128]{2,1,0:T(8,128)(2,1)S(1)}, f32[2,16,128]{2,1,0:T(8,128)S(1)}) custom-call(bf16[1,1,2,4,64,512]{5,4,3,2,1,0:T(8,128)(2,1)} %features_ref.1, bf16[432,512]{1,0:T(8,128)(2,1)} %bitcast.7, f32[1,16]{1,0:T(1,128)} %bitcast.8), custom_call_target="tpu_custom_call" | custom-call | tf_op jit(solution)/shard_map/conv/pallas_call | solution.py:301
  2.3 2.1 %collective-permute-start = (bf16[7,16,128]{2,1,0:T(8,128)(2,1)S(1)}, bf16[7,16,128]{2,1,0:T(8,128)(2,1)S(1)}, u32[]{:S(2)}, u32[]{:S(2)}) collective-permute-start(bf16[7,16,128]{2,1,0:T(8,128)(2,1)S(1)} %get-tuple-element.12.send_ref), channel_id=1, source_target_pairs={{0,16},{16,0},{1,17},{17,1},{2,18},{18,2},{3,19},{19,3},{4,20},{20... | collective-permute-start | bytes 86024 | tf_op jit(solution)/shard_map/ppermute | solution.py:309
  4.4 1.3 %collective-permute-done.recv_ref = bf16[7,16,128]{2,1,0:T(8,128)(2,1)S(1)} collective-permute-done((bf16[7,16,128]{2,1,0:T(8,128)(2,1)S(1)}, bf16[7,16,128]{2,1,0:T(8,128)(2,1)S(1)}, u32[]{:S(2)}, u32[]{:S(2)}) %collective-permute-start) | collective-permute-done | bytes 28704 | tf_op jit(solution)/shard_map/ppermute | solution.py:309
  5.6 0.2 finish.1.refs_0_
  5.8 3.2 %collective-permute-start.3 = (bf16[2,64,128]{2,1,0:T(8,128)(2,1)S(1)}, bf16[2,64,128]{2,1,0:T(8,128)(2,1)S(1)}, u32[]{:S(2)}, u32[]{:S(2)}) collective-permute-start(bf16[2,64,128]{2,1,0:T(8,128)(2,1)S(1)} %finish.1.refs_0_), channel_id=1, source_target_pairs={{0,3},{1,2},{2,1},{3,0},{4,7},{5,6},{6,5},{7,4},{8,11},{9,10},{10,... | collective-permute-start | bytes 98312 | tf_op jit(solution)/shard_map/ppermute | solution.py:361
  8.9 0.0 collective-permute-start.2
  9.0 0.5 %collective-permute-start.1 = (bf16[2,64,128]{2,1,0:T(8,128)(2,1)S(1)}, bf16[2,64,128]{2,1,0:T(8,128)(2,1)S(1)}, u32[]{:S(2)}, u32[]{:S(2)}) collective-permute-start(bf16[2,64,128]{2,1,0:T(8,128)(2,1)S(1)} %finish.1.refs_0_), channel_id=1, source_target_pairs={{0,1},{1,0},{2,3},{3,2},{4,5},{5,4},{6,7},{7,6},{8,9},{9,8},{10,11... | collective-permute-start | bytes 98312 | tf_op jit(solution)/shard_map/ppermute | solution.py:361
  9.4 0.0 copy-done
  9.4 0.9 %prepare.1 = (s32[2,2]{1,0:T(2,128)S(4)}, bf16[1536,64]{1,0:T(8,128)(2,1)S(1)}, f32[1,128]{1,0:T(1,128)S(1)}, f32[128,256]{1,0:T(8,128)S(1)}) custom-call(s32[4,4]{1,0:T(4,128)} %bucket_ref.1, s32[4,4]{1,0:T(4,128)} %frames_ref.1, bf16[64,4608]{1,0:T(8,128)(2,1)S(1)} %copy-done, f32[1,128]{1,0:T(1,128)} %bitcast.9, f32[1,128]{1,0:T(1,128)} %bitcast.10), custom_call_target="tpu_custom_call" | custom-call | tf_op jit(solution)/shard_map/prepare/pallas_call | solution.py:347
  10.4 0.2 %collective-permute-done.3.refs_3_ = bf16[2,64,128]{2,1,0:T(8,128)(2,1)S(1)} collective-permute-done((bf16[2,64,128]{2,1,0:T(8,128)(2,1)S(1)}, bf16[2,64,128]{2,1,0:T(8,128)(2,1)S(1)}, u32[]{:S(2)}, u32[]{:S(2)}) %collective-permute-start.3) | collective-permute-done | bytes 32800 | tf_op jit(solution)/shard_map/ppermute | solution.py:361
  10.5 1.2 %collective-permute-done.2.refs_2_ = bf16[2,64,128]{2,1,0:T(8,128)(2,1)S(1)} collective-permute-done((bf16[2,64,128]{2,1,0:T(8,128)(2,1)S(1)}, bf16[2,64,128]{2,1,0:T(8,128)(2,1)S(1)}, u32[]{:S(2)}, u32[]{:S(2)}) %collective-permute-start.2) | collective-permute-done | bytes 32800 | tf_op jit(solution)/shard_map/ppermute | solution.py:361
  11.7 0.0 collective-permute-done.1.refs_1_
  11.7 4.7 %attend.1 = bf16[2,128,1536]{2,1,0:T(8,128)(2,1)} custom-call(s32[2,2]{1,0:T(2,128)S(4)} %get-tuple-element.11.slot_ref, bf16[2,64,128]{2,1,0:T(8,128)(2,1)S(1)} %finish.1.refs_0_, bf16[2,64,128]{2,1,0:T(8,128)(2,1)S(1)} %collective-permute-done.1.refs_1_, bf16[2,64,128]{2,1,0:T(8,128)(2,1)S(1)} %collective-permute-done.2.refs_2_, ...), custom_call_target="tpu_custom_call" | custom-call | tf_op jit(solution)/shard_map/attend/pallas_call | solution.py:366
Async XLA Ops:
  0.0 9.4 %copy-start = (bf16[64,4608]{1,0:T(8,128)(2,1)S(1)}, bf16[64,4608]{1,0:T(8,128)(2,1)}, u32[]{:S(2)}) copy-start(bf16[64,4608]{1,0:T(8,128)(2,1)} %refs_4_.1) | copy-start | bytes 1769476
  2.3 3.4 %collective-permute-start = (bf16[7,16,128]{2,1,0:T(8,128)(2,1)S(1)}, bf16[7,16,128]{2,1,0:T(8,128)(2,1)S(1)}, u32[]{:S(2)}, u32[]{:S(2)}) collective-permute-start(bf16[7,16,128]{2,1,0:T(8,128)(2,1)S(1)} %get-tuple-element.12.send_ref), channel_id=1, source_target_pairs={{0,16},{16,0},{1,17},{17,1},{2,18},{18,2},{3,19},{19,3},{4,20},{20... | collective-permute-start | bytes 86024 | tf_op jit(solution)/shard_map/ppermute | solution.py:309
  5.8 4.7 %collective-permute-start.3 = (bf16[2,64,128]{2,1,0:T(8,128)(2,1)S(1)}, bf16[2,64,128]{2,1,0:T(8,128)(2,1)S(1)}, u32[]{:S(2)}, u32[]{:S(2)}) collective-permute-start(bf16[2,64,128]{2,1,0:T(8,128)(2,1)S(1)} %finish.1.refs_0_), channel_id=1, source_target_pairs={{0,3},{1,2},{2,1},{3,0},{4,7},{5,6},{6,5},{7,4},{8,11},{9,10},{10,... | collective-permute-start | bytes 98312 | tf_op jit(solution)/shard_map/ppermute | solution.py:361
  8.9 2.8 %collective-permute-start.2 = (bf16[2,64,128]{2,1,0:T(8,128)(2,1)S(1)}, bf16[2,64,128]{2,1,0:T(8,128)(2,1)S(1)}, u32[]{:S(2)}, u32[]{:S(2)}) collective-permute-start(bf16[2,64,128]{2,1,0:T(8,128)(2,1)S(1)} %finish.1.refs_0_), channel_id=1, source_target_pairs={{0,2},{1,3},{2,0},{3,1},{4,6},{5,7},{6,4},{7,5},{8,10},{9,11},{10,... | collective-permute-start | bytes 98312 | tf_op jit(solution)/shard_map/ppermute | solution.py:361
  9.0 2.8 %collective-permute-start.1 = (bf16[2,64,128]{2,1,0:T(8,128)(2,1)S(1)}, bf16[2,64,128]{2,1,0:T(8,128)(2,1)S(1)}, u32[]{:S(2)}, u32[]{:S(2)}) collective-permute-start(bf16[2,64,128]{2,1,0:T(8,128)(2,1)S(1)} %finish.1.refs_0_), channel_id=1, source_target_pairs={{0,1},{1,0},{2,3},{3,2},{4,5},{5,4},{6,7},{7,6},{8,9},{9,8},{10,11... | collective-permute-start | bytes 98312 | tf_op jit(solution)/shard_map/ppermute | solution.py:361

commit v3 on v2

--- a/solution.py
+++ b/solution.py
@@ -227,59 +227,72 @@
     pairs = HEADS // 2
     steps = CAP * pairs
 
-    def project(step):
+    def project_k(step, half):
+        slot, pair = divmod(step, pairs)
+        start = (2 * pair + half) * HEAD
+        k = jnp.dot(key_t_ref[start : start + HEAD, :], tr_scr[slot], preferred_element_type=F32)
+        k = k * lax.rsqrt(jnp.sum(k * k, axis=0, keepdims=True) + HEAD * EPS) * kscale_ref[...]
+        k_scr[step % 2, half] = k.astype(BF16)
+
+    def project_q(step):
         slot, pair = divmod(step, pairs)
         span = slice(pair * 2 * HEAD, (pair + 1) * 2 * HEAD)
         mine = nat_scr[slot, pl.ds(pl.multiple_of(tile * lanes, lanes), lanes), :]
         queries = jnp.dot(mine, embed_ref[:, span], preferred_element_type=F32)
         for half in range(2):
-            one = slice(half * HEAD, (half + 1) * HEAD)
-            k = jnp.dot(
-                key_t_ref[span.start + one.start : span.start + one.stop, :],
-                tr_scr[slot],
-                preferred_element_type=F32,
-            )
-            k = k * lax.rsqrt(jnp.sum(k * k, axis=0, keepdims=True) + HEAD * EPS) * kscale_ref[...]
-            k_scr[step % 2, half] = k.astype(BF16)
-            q = queries[:, one]
+            q = queries[:, half * HEAD : (half + 1) * HEAD]
             q = q * lax.rsqrt(jnp.sum(q * q, axis=1, keepdims=True) + HEAD * EPS) * qscale_ref[...]
             q_scr[step % 2, half] = q.astype(BF16)
+
+    def project_v(step):
+        slot, pair = divmod(step, pairs)
+        start = 2 * D + pair * 2 * HEAD
         v_scr[step % 3] = jnp.dot(
-            nat_scr[slot], embed_ref[:, 2 * D + span.start : 2 * D + span.stop], preferred_element_type=F32
+            nat_scr[slot], embed_ref[:, start : start + 2 * HEAD], preferred_element_type=F32
         ).astype(BF16)
 
-    def score(step):
+    def score(step, half):
         slot = step // pairs
-        for half in range(2):
-            scores = jnp.dot(q_scr[step % 2, half], k_scr[step % 2, half], preferred_element_type=F32)
-            weights = jnp.exp2(scores)
-            p_scr[step % 2, half] = weights.astype(BF16)
-            folded = weights[:, :lanes]
-            for t in range(1, tiles):
-                folded = folded + weights[:, t * lanes : (t + 1) * lanes]
-            totals = jnp.sum(folded * counted[slot], axis=1, keepdims=True)
-            r_scr[step % 2, half] = row_keep[slot] / totals
-
-    def mix(step):
+        scores = jnp.dot(q_scr[step % 2, half], k_scr[step % 2, half], preferred_element_type=F32)
+        weights = jnp.exp2(scores)
+        p_scr[step % 2, half] = weights.astype(BF16)
+        folded = weights[:, :lanes]
+        for t in range(1, tiles):
+            folded = folded + weights[:, t * lanes : (t + 1) * lanes]
+        totals = jnp.sum(folded * counted[slot], axis=1, keepdims=True)
+        r_scr[step % 2, half] = jnp.broadcast_to(row_keep[slot] / totals, (lanes, HEAD))
+
+    def mix(step, half):
         slot, pair = divmod(step, pairs)
-        for half in range(2):
-            one = slice(half * HEAD, (half + 1) * HEAD)
-            mixed = jnp.dot(p_scr[step % 2, half], v_scr[step % 3, :, one], preferred_element_type=F32)
-            start = pair * 2 * HEAD + one.start
-            out_scr[slot, :, start : start + HEAD] = (mixed * r_scr[step % 2, half]).astype(BF16)
+        start = (2 * pair + half) * HEAD
+        mixed = jnp.dot(
+            p_scr[step % 2, half], v_scr[step % 3, :, half * HEAD : (half + 1) * HEAD], preferred_element_type=F32
+        )
+        out_scr[slot, :, start : start + HEAD] = (mixed * r_scr[step % 2, half]).astype(BF16)
+        if half == 1:
+            part = (slot, slice(None), pl.ds(pair * 2 * HEAD, 2 * HEAD))
+            copies.append(pltpu.make_async_copy(out_scr.at[part], out_ref.at[part], sem.at[step]))
+            copies[-1].start()
 
     copies = []
     for step in range(steps + 2):
-        if step >= 2:
-            mix(step - 2)
-            if (step - 1) % pairs == 0:
-                slot = (step - 2) // pairs
-                copies.append(pltpu.make_async_copy(out_scr.at[slot], out_ref.at[slot], sem.at[slot]))
-                copies[-1].start()
-        if 1 <= step <= steps:
-            score(step - 1)
-        if step < steps:
-            project(step)
+        here, last, before = step < steps, 1 <= step <= steps, step >= 2
+        if here:
+            project_q(step)
+        if here:
+            project_k(step, 0)
+        if here:
+            project_k(step, 1)
+        if here:
+            project_v(step)
+        if last:
+            score(step - 1, 0)
+        if last:
+            score(step - 1, 1)
+        if before:
+            mix(step - 2, 0)
+        if before:
+            mix(step - 2, 1)
     for copy in copies:
         copy.wait()
 
@@ -375,9 +388,9 @@
             pltpu.VMEM((2, 2, lanes, HEAD), BF16),
             pltpu.VMEM((3, clip, 2 * HEAD), BF16),
             pltpu.VMEM((2, 2, lanes, clip), BF16),
-            pltpu.VMEM((2, 2, lanes, 1), F32),
+            pltpu.VMEM((2, 2, lanes, HEAD), F32),
             pltpu.VMEM((CAP, lanes, D), BF16),
-            pltpu.SemaphoreType.DMA((CAP,)),
+            pltpu.SemaphoreType.DMA((CAP * HEADS // 2,)),
         ],
         name="attend",
     )(pltpu.with_memory_space_constraint(slots, pltpu.SMEM), *in_vmem(*sources, embed, key_t, query_scale, key_scale))

time: 16.6 us -> 15.1 us (0.910)
  Pallas kernels: 8.01 us -> 6.6 us
    pallas_call x1, Pallas kernels: 4.67 us -> 3.25 us  [shards(): pl.pallas_call(functools.partial(attend_kernel, sources=len(sources), col...]
where the time goes in v3:
time: 15.1 us; the launch traced here: 15 us
  Pallas kernels  6.6 us (44%)
  starting transfers between devices  5.74 us (38%)
  waiting for transfers between devices  2.61 us (17%)
    ppermute x3, starting transfers between devices, shards(): lax.ppermute(tokens, 'group', [(i, i ^ k) for i in range(groups)])  3.61 us
    pallas_call x1, Pallas kernels, shards(): pl.pallas_call(functools.partial(attend_kernel, sources=len(sources), col...  3.25 us
    pallas_call x1, Pallas kernels, clip_tokens(): pl.pallas_call(conv_pair_kernel, out_shape=(pltpu.VMEM((rows + 3, zc, lan...  2.25 us
    ppermute x1, starting transfers between devices, clip_tokens(): recv = lax.ppermute(send, 'tile', [(0, 1), (1, 0)])  2.12 us
    ppermute x3, waiting for transfers between devices, shards(): lax.ppermute(tokens, 'group', [(i, i ^ k) for i in range(groups)])  1.35 us
    ppermute x1, waiting for transfers between devices, clip_tokens(): recv = lax.ppermute(send, 'tile', [(0, 1), (1, 0)])  1.26 us
    pallas_call x1, Pallas kernels, shards(): pl.pallas_call(prepare_kernel, out_shape=(pltpu.SMEM((2, CAP), jnp.int32)...  0.94 us
  transfers between devices with their start and end apart: 4, of which 3 were waited for; matrix products, arithmetic and copies ran while one was open for 0% of the time, Pallas kernels for 6%

profile of v3, /device:TPU:1, one launch (start us, length us, event | category | flops | bytes accessed | tf_op | source)
XLA Modules:
  0.0 15.0 jit_solution(1386529574660990149)
XLA Ops:
  0.0 0.0 copy-start
  0.0 2.2 %conv.1 = (bf16[7,16,128]{2,1,0:T(8,128)(2,1)S(1)}, f32[2,16,128]{2,1,0:T(8,128)S(1)}) custom-call(bf16[1,1,2,4,64,512]{5,4,3,2,1,0:T(8,128)(2,1)} %features_ref.1, bf16[432,512]{1,0:T(8,128)(2,1)} %bitcast.7, f32[1,16]{1,0:T(1,128)} %bitcast.8), custom_call_target="tpu_custom_call" | custom-call | tf_op jit(solution)/shard_map/conv/pallas_call | solution.py:314
  2.3 2.1 %collective-permute-start = (bf16[7,16,128]{2,1,0:T(8,128)(2,1)S(1)}, bf16[7,16,128]{2,1,0:T(8,128)(2,1)S(1)}, u32[]{:S(2)}, u32[]{:S(2)}) collective-permute-start(bf16[7,16,128]{2,1,0:T(8,128)(2,1)S(1)} %get-tuple-element.12.send_ref), channel_id=1, source_target_pairs={{0,16},{16,0},{1,17},{17,1},{2,18},{18,2},{3,19},{19,3},{4,20},{20... | collective-permute-start | bytes 86024 | tf_op jit(solution)/shard_map/ppermute | solution.py:322
  4.4 1.3 %collective-permute-done.recv_ref = bf16[7,16,128]{2,1,0:T(8,128)(2,1)S(1)} collective-permute-done((bf16[7,16,128]{2,1,0:T(8,128)(2,1)S(1)}, bf16[7,16,128]{2,1,0:T(8,128)(2,1)S(1)}, u32[]{:S(2)}, u32[]{:S(2)}) %collective-permute-start) | collective-permute-done | bytes 28704 | tf_op jit(solution)/shard_map/ppermute | solution.py:322
  5.6 0.2 %finish.1.refs_0_ = bf16[2,64,128]{2,1,0:T(8,128)(2,1)S(1)} custom-call(bf16[7,16,128]{2,1,0:T(8,128)(2,1)S(1)} %get-tuple-element.12.send_ref, bf16[7,16,128]{2,1,0:T(8,128)(2,1)S(1)} %collective-permute-done.recv_ref, f32[2,16,128]{2,1,0:T(8,128)S(1)} %get-tuple-element.13.keep_ref), custom_call_target="tpu_custom_call" | custom-call | tf_op jit(solution)/shard_map/finish/pallas_call | solution.py:323
  5.8 3.2 %collective-permute-start.3 = (bf16[2,64,128]{2,1,0:T(8,128)(2,1)S(1)}, bf16[2,64,128]{2,1,0:T(8,128)(2,1)S(1)}, u32[]{:S(2)}, u32[]{:S(2)}) collective-permute-start(bf16[2,64,128]{2,1,0:T(8,128)(2,1)S(1)} %finish.1.refs_0_), channel_id=1, source_target_pairs={{0,3},{1,2},{2,1},{3,0},{4,7},{5,6},{6,5},{7,4},{8,11},{9,10},{10,... | collective-permute-start | bytes 98312 | tf_op jit(solution)/shard_map/ppermute | solution.py:374
  8.9 0.0 collective-permute-start.2
  9.0 0.5 %collective-permute-start.1 = (bf16[2,64,128]{2,1,0:T(8,128)(2,1)S(1)}, bf16[2,64,128]{2,1,0:T(8,128)(2,1)S(1)}, u32[]{:S(2)}, u32[]{:S(2)}) collective-permute-start(bf16[2,64,128]{2,1,0:T(8,128)(2,1)S(1)} %finish.1.refs_0_), channel_id=1, source_target_pairs={{0,1},{1,0},{2,3},{3,2},{4,5},{5,4},{6,7},{7,6},{8,9},{9,8},{10,11... | collective-permute-start | bytes 98312 | tf_op jit(solution)/shard_map/ppermute | solution.py:374
  9.4 0.0 copy-done
  9.4 0.9 %prepare.1 = (s32[2,2]{1,0:T(2,128)S(4)}, bf16[1536,64]{1,0:T(8,128)(2,1)S(1)}, f32[1,128]{1,0:T(1,128)S(1)}, f32[128,256]{1,0:T(8,128)S(1)}) custom-call(s32[4,4]{1,0:T(4,128)} %bucket_ref.1, s32[4,4]{1,0:T(4,128)} %frames_ref.1, bf16[64,4608]{1,0:T(8,128)(2,1)S(1)} %copy-done, f32[1,128]{1,0:T(1,128)} %bitcast.9, f32[1,128]{1,0:T(1,128)} %bitcast.10), custom_call_target="tpu_custom_call" | custom-call | tf_op jit(solution)/shard_map/prepare/pallas_call | solution.py:360
  10.4 0.2 %collective-permute-done.3.refs_3_ = bf16[2,64,128]{2,1,0:T(8,128)(2,1)S(1)} collective-permute-done((bf16[2,64,128]{2,1,0:T(8,128)(2,1)S(1)}, bf16[2,64,128]{2,1,0:T(8,128)(2,1)S(1)}, u32[]{:S(2)}, u32[]{:S(2)}) %collective-permute-start.3) | collective-permute-done | bytes 32800 | tf_op jit(solution)/shard_map/ppermute | solution.py:374
  10.5 1.2 %collective-permute-done.2.refs_2_ = bf16[2,64,128]{2,1,0:T(8,128)(2,1)S(1)} collective-permute-done((bf16[2,64,128]{2,1,0:T(8,128)(2,1)S(1)}, bf16[2,64,128]{2,1,0:T(8,128)(2,1)S(1)}, u32[]{:S(2)}, u32[]{:S(2)}) %collective-permute-start.2) | collective-permute-done | bytes 32800 | tf_op jit(solution)/shard_map/ppermute | solution.py:374
  11.7 0.0 collective-permute-done.1.refs_1_
  11.7 3.3 %attend.1 = bf16[2,128,1536]{2,1,0:T(8,128)(2,1)} custom-call(s32[2,2]{1,0:T(2,128)S(4)} %get-tuple-element.11.slot_ref, bf16[2,64,128]{2,1,0:T(8,128)(2,1)S(1)} %finish.1.refs_0_, bf16[2,64,128]{2,1,0:T(8,128)(2,1)S(1)} %collective-permute-done.1.refs_1_, bf16[2,64,128]{2,1,0:T(8,128)(2,1)S(1)} %collective-permute-done.2.refs_2_, ...), custom_call_target="tpu_custom_call" | custom-call | tf_op jit(solution)/shard_map/attend/pallas_call | solution.py:379
Async XLA Ops:
  0.0 9.4 %copy-start = (bf16[64,4608]{1,0:T(8,128)(2,1)S(1)}, bf16[64,4608]{1,0:T(8,128)(2,1)}, u32[]{:S(2)}) copy-start(bf16[64,4608]{1,0:T(8,128)(2,1)} %refs_4_.1) | copy-start | bytes 1769476
  2.3 3.4 %collective-permute-start = (bf16[7,16,128]{2,1,0:T(8,128)(2,1)S(1)}, bf16[7,16,128]{2,1,0:T(8,128)(2,1)S(1)}, u32[]{:S(2)}, u32[]{:S(2)}) collective-permute-start(bf16[7,16,128]{2,1,0:T(8,128)(2,1)S(1)} %get-tuple-element.12.send_ref), channel_id=1, source_target_pairs={{0,16},{16,0},{1,17},{17,1},{2,18},{18,2},{3,19},{19,3},{4,20},{20... | collective-permute-start | bytes 86024 | tf_op jit(solution)/shard_map/ppermute | solution.py:322
  5.8 4.7 %collective-permute-start.3 = (bf16[2,64,128]{2,1,0:T(8,128)(2,1)S(1)}, bf16[2,64,128]{2,1,0:T(8,128)(2,1)S(1)}, u32[]{:S(2)}, u32[]{:S(2)}) collective-permute-start(bf16[2,64,128]{2,1,0:T(8,128)(2,1)S(1)} %finish.1.refs_0_), channel_id=1, source_target_pairs={{0,3},{1,2},{2,1},{3,0},{4,7},{5,6},{6,5},{7,4},{8,11},{9,10},{10,... | collective-permute-start | bytes 98312 | tf_op jit(solution)/shard_map/ppermute | solution.py:374
  8.9 2.8 %collective-permute-start.2 = (bf16[2,64,128]{2,1,0:T(8,128)(2,1)S(1)}, bf16[2,64,128]{2,1,0:T(8,128)(2,1)S(1)}, u32[]{:S(2)}, u32[]{:S(2)}) collective-permute-start(bf16[2,64,128]{2,1,0:T(8,128)(2,1)S(1)} %finish.1.refs_0_), channel_id=1, source_target_pairs={{0,2},{1,3},{2,0},{3,1},{4,6},{5,7},{6,4},{7,5},{8,10},{9,11},{10,... | collective-permute-start | bytes 98312 | tf_op jit(solution)/shard_map/ppermute | solution.py:374
  9.0 2.8 %collective-permute-start.1 = (bf16[2,64,128]{2,1,0:T(8,128)(2,1)S(1)}, bf16[2,64,128]{2,1,0:T(8,128)(2,1)S(1)}, u32[]{:S(2)}, u32[]{:S(2)}) collective-permute-start(bf16[2,64,128]{2,1,0:T(8,128)(2,1)S(1)} %finish.1.refs_0_), channel_id=1, source_target_pairs={{0,1},{1,0},{2,3},{3,2},{4,5},{5,4},{6,7},{7,6},{8,9},{9,8},{10,11... | collective-permute-start | bytes 98312 | tf_op jit(solution)/shard_map/ppermute | solution.py:374

commit v4 on v3

--- a/solution.py
+++ b/solution.py
@@ -87,25 +87,31 @@
     def add(*parts):
         return [tuple(sum(p[c][k] for p in parts) for k in range(2)) for c in range(3)]
 
+    def where(flag, one, other):
+        return [
+            tuple(jnp.where(flag, one[c][k], 0.0 if other is None else other[c][k]) for k in range(2))
+            for c in range(3)
+        ]
+
     out = []
     for row in range(rows):
         parts = [taps[row + b - 1][b] for b in range(3) if 0 <= row + b - 1 < rows]
-        value = finish(add(*parts)) + bias
         if row == 0:
-            value = value + jnp.where(is_first, finish(taps[0][0]), 0.0)
+            parts.append(where(is_first, taps[0][0], None))
         if row == rows - 1:
-            value = value + jnp.where(is_last, finish(taps[rows - 1][2]), 0.0)
-        out.append(value)
-    return out, finish(taps[rows - 1][0]), finish(taps[0][2]), is_first
+            parts.append(where(is_last, taps[rows - 1][2], None))
+        out.append(finish(add(*parts)) + bias)
+    if tiles == 2:
+        return out, (finish(where(is_first, taps[rows - 1][0], taps[0][2])),), is_first
+    return out, (finish(taps[rows - 1][0]), finish(taps[0][2])), is_first
 
 
 def conv_pair_kernel(features_ref, weight_ref, bias_ref, send_ref, keep_ref, *scratch):
-    out, below, above, is_first = conv_rows(features_ref, weight_ref, bias_ref, *scratch, 2)
+    out, (owed,), is_first = conv_rows(features_ref, weight_ref, bias_ref, *scratch, 2)
     rows = len(out)
     for row in range(rows):
         send_ref[row] = out[row].astype(BF16)
     edge = jnp.where(is_first, out[rows - 1], out[0])
-    owed = jnp.where(is_first, below, above)
     keep_ref[0] = edge
     keep_ref[1] = owed
     send_ref[rows] = (edge - edge.astype(BF16).astype(F32)).astype(BF16)
@@ -159,11 +165,11 @@
 
 
 def conv_any_kernel(features_ref, weight_ref, bias_ref, part_ref, owed_ref, *scratch, tiles):
-    out, below, above, _ = conv_rows(features_ref, weight_ref, bias_ref, *scratch, tiles)
+    out, owed, _ = conv_rows(features_ref, weight_ref, bias_ref, *scratch, tiles)
     for row, value in enumerate(out):
         part_ref[row] = value
-    owed_ref[0] = below
-    owed_ref[1] = above
+    owed_ref[0] = owed[0]
+    owed_ref[1] = owed[1]
 
 
 def finish_any_kernel(part_ref, from_low_ref, from_high_ref, tokens_ref, *, cols):
@@ -225,7 +231,6 @@
         tr_scr[slot] = tokens_t.astype(BF16)
 
     pairs = HEADS // 2
-    steps = CAP * pairs
 
     def project_k(step, half):
         slot, pair = divmod(step, pairs)
@@ -275,26 +280,39 @@
             copies[-1].start()
 
     copies = []
-    for step in range(steps + 2):
-        here, last, before = step < steps, 1 <= step <= steps, step >= 2
-        if here:
-            project_q(step)
-        if here:
-            project_k(step, 0)
-        if here:
-            project_k(step, 1)
-        if here:
-            project_v(step)
-        if last:
-            score(step - 1, 0)
-        if last:
-            score(step - 1, 1)
-        if before:
-            mix(step - 2, 0)
-        if before:
-            mix(step - 2, 1)
-    for copy in copies:
-        copy.wait()
+
+    def run(slots):
+        steps = slots * pairs
+        for slot in range(slots, CAP):
+            out_scr[slot] = jnp.zeros(out_scr.shape[1:], BF16)
+            copies.append(pltpu.make_async_copy(out_scr.at[slot], out_ref.at[slot], sem.at[slot * pairs]))
+            copies[-1].start()
+        for step in range(steps + 2):
+            here, last, before = step < steps, 1 <= step <= steps, step >= 2
+            if here:
+                project_q(step)
+                project_k(step, 0)
+                project_k(step, 1)
+                project_v(step)
+            if last:
+                score(step - 1, 0)
+                score(step - 1, 1)
+            if before:
+                mix(step - 2, 0)
+                mix(step - 2, 1)
+        for copy in copies:
+            copy.wait()
+        copies.clear()
+
+    double = slot_ref[1, CAP - 1] > 0
+
+    @pl.when(double)
+    def _():
+        run(CAP)
+
+    @pl.when(jnp.logical_not(double))
+    def _():
+        run(1)
 
 
 def clip_tokens(features, weight_t, bias_row):

time: 15.1 us -> 14.2 us (0.940)
  Pallas kernels: 6.6 us -> 5.56 us
    pallas_call x1, Pallas kernels: 3.25 us -> 2.22 us  [shards(): pl.pallas_call(functools.partial(attend_kernel, sources=len(sources), col...]
  transfers between devices with their start and end apart: 4 -> 4, of which waited for: 3 -> 3; matrix products, arithmetic and copies ran while one was open for 0% -> 0% of each run, Pallas kernels for 6% -> 7%
where the time goes in v4:
time: 14.2 us; the launch traced here: 13.9 us
  starting transfers between devices  5.74 us (40%)
  Pallas kernels  5.56 us (39%)
  waiting for transfers between devices  2.61 us (18%)
    ppermute x3, starting transfers between devices, shards(): lax.ppermute(tokens, 'group', [(i, i ^ k) for i in range(groups)])  3.61 us
    pallas_call x1, Pallas kernels, clip_tokens(): pl.pallas_call(conv_pair_kernel, out_shape=(pltpu.VMEM((rows + 3, zc, lan...  2.25 us
    pallas_call x1, Pallas kernels, shards(): pl.pallas_call(functools.partial(attend_kernel, sources=len(sources), col...  2.22 us
    ppermute x1, starting transfers between devices, clip_tokens(): recv = lax.ppermute(send, 'tile', [(0, 1), (1, 0)])  2.12 us
    ppermute x3, waiting for transfers between devices, shards(): lax.ppermute(tokens, 'group', [(i, i ^ k) for i in range(groups)])  1.35 us
    ppermute x1, waiting for transfers between devices, clip_tokens(): recv = lax.ppermute(send, 'tile', [(0, 1), (1, 0)])  1.26 us
    pallas_call x1, Pallas kernels, shards(): pl.pallas_call(prepare_kernel, out_shape=(pltpu.SMEM((2, CAP), jnp.int32)...  0.94 us
  transfers between devices with their start and end apart: 4, of which 3 were waited for; matrix products, arithmetic and copies ran while one was open for 0% of the time, Pallas kernels for 7%

profile of v4, /device:TPU:1, one launch (start us, length us, event | category | flops | bytes accessed | tf_op | source)
XLA Modules:
  0.0 13.9 jit_solution(17344222835926629383)
XLA Ops:
  0.0 0.0 copy-start
  0.0 2.2 %conv.1 = (bf16[7,16,128]{2,1,0:T(8,128)(2,1)S(1)}, f32[2,16,128]{2,1,0:T(8,128)S(1)}) custom-call(bf16[1,1,2,4,64,512]{5,4,3,2,1,0:T(8,128)(2,1)} %features_ref.1, bf16[432,512]{1,0:T(8,128)(2,1)} %bitcast.7, f32[1,16]{1,0:T(1,128)} %bitcast.8), custom_call_target="tpu_custom_call" | custom-call | tf_op jit(solution)/shard_map/conv/pallas_call | solution.py:332
  2.3 2.1 %collective-permute-start = (bf16[7,16,128]{2,1,0:T(8,128)(2,1)S(1)}, bf16[7,16,128]{2,1,0:T(8,128)(2,1)S(1)}, u32[]{:S(2)}, u32[]{:S(2)}) collective-permute-start(bf16[7,16,128]{2,1,0:T(8,128)(2,1)S(1)} %get-tuple-element.12.send_ref), channel_id=1, source_target_pairs={{0,16},{16,0},{1,17},{17,1},{2,18},{18,2},{3,19},{19,3},{4,20},{20... | collective-permute-start | bytes 86024 | tf_op jit(solution)/shard_map/ppermute | solution.py:340
  4.4 1.3 %collective-permute-done.recv_ref = bf16[7,16,128]{2,1,0:T(8,128)(2,1)S(1)} collective-permute-done((bf16[7,16,128]{2,1,0:T(8,128)(2,1)S(1)}, bf16[7,16,128]{2,1,0:T(8,128)(2,1)S(1)}, u32[]{:S(2)}, u32[]{:S(2)}) %collective-permute-start) | collective-permute-done | bytes 28704 | tf_op jit(solution)/shard_map/ppermute | solution.py:340
  5.6 0.2 %finish.1.refs_0_ = bf16[2,64,128]{2,1,0:T(8,128)(2,1)S(1)} custom-call(bf16[7,16,128]{2,1,0:T(8,128)(2,1)S(1)} %get-tuple-element.12.send_ref, bf16[7,16,128]{2,1,0:T(8,128)(2,1)S(1)} %collective-permute-done.recv_ref, f32[2,16,128]{2,1,0:T(8,128)S(1)} %get-tuple-element.13.keep_ref), custom_call_target="tpu_custom_call" | custom-call | tf_op jit(solution)/shard_map/finish/pallas_call | solution.py:341
  5.8 3.2 %collective-permute-start.3 = (bf16[2,64,128]{2,1,0:T(8,128)(2,1)S(1)}, bf16[2,64,128]{2,1,0:T(8,128)(2,1)S(1)}, u32[]{:S(2)}, u32[]{:S(2)}) collective-permute-start(bf16[2,64,128]{2,1,0:T(8,128)(2,1)S(1)} %finish.1.refs_0_), channel_id=1, source_target_pairs={{0,3},{1,2},{2,1},{3,0},{4,7},{5,6},{6,5},{7,4},{8,11},{9,10},{10,... | collective-permute-start | bytes 98312 | tf_op jit(solution)/shard_map/ppermute | solution.py:392
  9.0 0.0 collective-permute-start.2
  9.0 0.5 %collective-permute-start.1 = (bf16[2,64,128]{2,1,0:T(8,128)(2,1)S(1)}, bf16[2,64,128]{2,1,0:T(8,128)(2,1)S(1)}, u32[]{:S(2)}, u32[]{:S(2)}) collective-permute-start(bf16[2,64,128]{2,1,0:T(8,128)(2,1)S(1)} %finish.1.refs_0_), channel_id=1, source_target_pairs={{0,1},{1,0},{2,3},{3,2},{4,5},{5,4},{6,7},{7,6},{8,9},{9,8},{10,11... | collective-permute-start | bytes 98312 | tf_op jit(solution)/shard_map/ppermute | solution.py:392
  9.4 0.0 copy-done
  9.4 0.9 %prepare.1 = (s32[2,2]{1,0:T(2,128)S(4)}, bf16[1536,64]{1,0:T(8,128)(2,1)S(1)}, f32[1,128]{1,0:T(1,128)S(1)}, f32[128,256]{1,0:T(8,128)S(1)}) custom-call(s32[4,4]{1,0:T(4,128)} %bucket_ref.1, s32[4,4]{1,0:T(4,128)} %frames_ref.1, bf16[64,4608]{1,0:T(8,128)(2,1)S(1)} %copy-done, f32[1,128]{1,0:T(1,128)} %bitcast.9, f32[1,128]{1,0:T(1,128)} %bitcast.10), custom_call_target="tpu_custom_call" | custom-call | tf_op jit(solution)/shard_map/prepare/pallas_call | solution.py:378
  10.4 0.2 %collective-permute-done.3.refs_3_ = bf16[2,64,128]{2,1,0:T(8,128)(2,1)S(1)} collective-permute-done((bf16[2,64,128]{2,1,0:T(8,128)(2,1)S(1)}, bf16[2,64,128]{2,1,0:T(8,128)(2,1)S(1)}, u32[]{:S(2)}, u32[]{:S(2)}) %collective-permute-start.3) | collective-permute-done | bytes 32800 | tf_op jit(solution)/shard_map/ppermute | solution.py:392
  10.5 1.2 %collective-permute-done.2.refs_2_ = bf16[2,64,128]{2,1,0:T(8,128)(2,1)S(1)} collective-permute-done((bf16[2,64,128]{2,1,0:T(8,128)(2,1)S(1)}, bf16[2,64,128]{2,1,0:T(8,128)(2,1)S(1)}, u32[]{:S(2)}, u32[]{:S(2)}) %collective-permute-start.2) | collective-permute-done | bytes 32800 | tf_op jit(solution)/shard_map/ppermute | solution.py:392
  11.7 0.0 collective-permute-done.1.refs_1_
  11.7 2.2 %attend.1 = bf16[2,128,1536]{2,1,0:T(8,128)(2,1)} custom-call(s32[2,2]{1,0:T(2,128)S(4)} %get-tuple-element.11.slot_ref, bf16[2,64,128]{2,1,0:T(8,128)(2,1)S(1)} %finish.1.refs_0_, bf16[2,64,128]{2,1,0:T(8,128)(2,1)S(1)} %collective-permute-done.1.refs_1_, bf16[2,64,128]{2,1,0:T(8,128)(2,1)S(1)} %collective-permute-done.2.refs_2_, ...), custom_call_target="tpu_custom_call" | custom-call | tf_op jit(solution)/shard_map/attend/pallas_call | solution.py:397
Async XLA Ops:
  0.0 9.4 %copy-start = (bf16[64,4608]{1,0:T(8,128)(2,1)S(1)}, bf16[64,4608]{1,0:T(8,128)(2,1)}, u32[]{:S(2)}) copy-start(bf16[64,4608]{1,0:T(8,128)(2,1)} %refs_4_.1) | copy-start | bytes 1769476
  2.3 3.4 %collective-permute-start = (bf16[7,16,128]{2,1,0:T(8,128)(2,1)S(1)}, bf16[7,16,128]{2,1,0:T(8,128)(2,1)S(1)}, u32[]{:S(2)}, u32[]{:S(2)}) collective-permute-start(bf16[7,16,128]{2,1,0:T(8,128)(2,1)S(1)} %get-tuple-element.12.send_ref), channel_id=1, source_target_pairs={{0,16},{16,0},{1,17},{17,1},{2,18},{18,2},{3,19},{19,3},{4,20},{20... | collective-permute-start | bytes 86024 | tf_op jit(solution)/shard_map/ppermute | solution.py:340
  5.8 4.7 %collective-permute-start.3 = (bf16[2,64,128]{2,1,0:T(8,128)(2,1)S(1)}, bf16[2,64,128]{2,1,0:T(8,128)(2,1)S(1)}, u32[]{:S(2)}, u32[]{:S(2)}) collective-permute-start(bf16[2,64,128]{2,1,0:T(8,128)(2,1)S(1)} %finish.1.refs_0_), channel_id=1, source_target_pairs={{0,3},{1,2},{2,1},{3,0},{4,7},{5,6},{6,5},{7,4},{8,11},{9,10},{10,... | collective-permute-start | bytes 98312 | tf_op jit(solution)/shard_map/ppermute | solution.py:392
  9.0 2.8 %collective-permute-start.2 = (bf16[2,64,128]{2,1,0:T(8,128)(2,1)S(1)}, bf16[2,64,128]{2,1,0:T(8,128)(2,1)S(1)}, u32[]{:S(2)}, u32[]{:S(2)}) collective-permute-start(bf16[2,64,128]{2,1,0:T(8,128)(2,1)S(1)} %finish.1.refs_0_), channel_id=1, source_target_pairs={{0,2},{1,3},{2,0},{3,1},{4,6},{5,7},{6,4},{7,5},{8,10},{9,11},{10,... | collective-permute-start | bytes 98312 | tf_op jit(solution)/shard_map/ppermute | solution.py:392
  9.0 2.8 %collective-permute-start.1 = (bf16[2,64,128]{2,1,0:T(8,128)(2,1)S(1)}, bf16[2,64,128]{2,1,0:T(8,128)(2,1)S(1)}, u32[]{:S(2)}, u32[]{:S(2)}) collective-permute-start(bf16[2,64,128]{2,1,0:T(8,128)(2,1)S(1)} %finish.1.refs_0_), channel_id=1, source_target_pairs={{0,1},{1,0},{2,3},{3,2},{4,5},{5,4},{6,7},{7,6},{8,9},{9,8},{10,11... | collective-permute-start | bytes 98312 | tf_op jit(solution)/shard_map/ppermute | solution.py:392
